TPU v7x, 128 devices: a whole 4x4x4 slice. The times are simulated.
128 devices in a mesh: dp: 4 (over z_lo, core), seq: 8 (over x, z_hi), tensor: 4 (over y).
Axes of the slice: x: 4, y: 4, z: 4 (z_hi: 2, z_lo: 2; z = z_hi * 2 + z_lo), core: 2. Of those that a mesh axis runs over, the one named last changes fastest.
Arguments:
- latents: bfloat16 [4, 16, 256, 1152], P('dp', 'seq', 'tensor'), may hold values from -6 to 6
- modulation: float32 [4, 6, 1152], P('dp'), may hold values from -3 to 3
- in_weight: bfloat16 [1152, 3, 1152], P(None, None, 'tensor'), may hold values from -0.5 to 0.5
- out_weight: bfloat16 [1152, 1152], P('tensor'), may hold values from -0.1875 to 0.1875
- up_weight: bfloat16 [1152, 4608], P(None, 'tensor'), may hold values from -0.1875 to 0.1875
- down_weight: bfloat16 [4608, 1152], P('tensor'), may hold values from -0.09375 to 0.09375
- cotangent: bfloat16 [4, 16, 256, 1152], P('dp', 'seq', 'tensor'), may hold values from -6 to 6
Outputs:
- result: bfloat16 [4, 16, 256, 1152], P('dp', 'seq', 'tensor')
- latents_grad: bfloat16 [4, 16, 256, 1152], P('dp', 'seq', 'tensor')
- in_grad: bfloat16 [1152, 3, 1152], P(('dp', 'seq'), None, 'tensor')
- out_grad: bfloat16 [1152, 1152], P('tensor', ('dp', 'seq'))
- up_grad: bfloat16 [1152, 4608], P(('dp', 'seq'), 'tensor')
- down_grad: bfloat16 [4608, 1152], P('tensor', ('dp', 'seq'))
All inputs are finite; a program needn't handle non-finite values.
Results may differ from a plain program's by a relative error of at most 0.02.
The roundings to bfloat16 on the way count: a program that leaves them out, or rounds other values in their place, can miss the bound.
Values may be sent and summed in bfloat16 or wider, within the bound.
A program may use at most 128 MiB of HBM per device.

v0:
```python
import math

import jax
import jax.numpy as jnp
from jax import lax
from jax.sharding import PartitionSpec as P

HEAD_DIM = 72


epsilon = 1e-06


def from_everyone(array, axis):
    size = lax.axis_size(axis)
    return lax.all_to_all(
        jnp.broadcast_to(array[None], (size, *array.shape)), axis, 0, 0, tiled=True
    )


def laid_out(pieces, dim):
    lengths = list(pieces.shape[1:])
    lengths[dim] *= pieces.shape[0]
    return jnp.moveaxis(pieces, 0, dim).reshape(lengths)


def gathered_copies(array, axis, dim):
    pieces = from_everyone(array, axis)
    return laid_out(pieces, dim)


def cut_along(array, dim, size):
    before, after = (array.shape[:dim], array.shape[dim + 1 :])
    return jnp.moveaxis(array.reshape(*before, size, -1, *after), dim, 0)


def sent_and_summed(array, axis, dim):
    pieces = cut_along(array, dim, lax.axis_size(axis))
    arrived = lax.all_to_all(pieces, axis, split_axis=0, concat_axis=0, tiled=True)
    return arrived.astype(jnp.float32).sum(axis=0)


def in_one_piece(arrays, axis, dim, along):
    widths = [a.shape[along] for a in arrays]
    both = jnp.concatenate(arrays, axis=along)
    result = lax.psum_scatter(both, axis, scatter_dimension=dim, tiled=True)
    return tuple(jnp.split(result, [sum(widths[:k]) for k in range(1, len(widths))], axis=along))


def sum_packed(arrays, axis, dims):
    size = lax.axis_size(axis)
    pieces = [cut_along(a, dim, size) for a, dim in zip(arrays, dims)]
    lines = jnp.concatenate([b.reshape(size, -1) for b in pieces], axis=1)
    rows = max(16, -(-lines.shape[1] // 1024) * 8)
    lines = jnp.pad(lines, ((0, 0), (0, rows * 128 - lines.shape[1]))).reshape(-1, 128)
    line, at, finished = (lax.psum_scatter(lines, axis, tiled=True).reshape(-1), 0, [])
    for b in pieces:
        part = b[0]
        finished.append(line[at : at + part.size].reshape(part.shape))
        at += part.size
    return tuple(finished)


def normalize(rows):
    center = jnp.mean(rows, axis=-1, keepdims=True)
    centred = rows - center
    spread = jnp.mean(centred * centred, axis=-1, keepdims=True)
    inverse = lax.rsqrt(spread + epsilon)
    return (centred * inverse, inverse)


def norm_back(normed, inverse, upstream):
    mean_grad = jnp.mean(upstream, axis=-1, keepdims=True)
    mean_cross = jnp.mean(upstream * normed, axis=-1, keepdims=True)
    return (upstream - mean_grad - normed * mean_cross) * inverse


def gelu_tanh(values):
    return jax.nn.gelu(values, approximate=True)


def flat_dot(left, right):
    leading = left.shape[:-1]
    out_rows = jnp.dot(left.reshape(-1, left.shape[-1]), right, preferred_element_type=jnp.float32)
    return out_rows.reshape(leading + (right.shape[-1],))


def flat_dot_t(left, right):
    leading = left.shape[:-1]
    out_rows = lax.dot_general(
        left.reshape(-1, left.shape[-1]),
        right,
        (((1,), (1,)), ((), ())),
        preferred_element_type=jnp.float32,
    )
    return out_rows.reshape(leading + (right.shape[0],))


def weight_grad(left, right):
    return lax.dot_general(
        left.reshape(-1, left.shape[-1]),
        right.reshape(-1, right.shape[-1]),
        (((0,), (0,)), ((), ())),
        preferred_element_type=jnp.float32,
    )


def attend(queries, key_rows, value_rows):
    scaling = 1.0 / math.sqrt(queries.shape[-1])
    scores = (
        jnp.einsum("bfphe,bgphe->bphfg", queries, key_rows, preferred_element_type=jnp.float32)
        * scaling
    )
    highest = jnp.max(scores, axis=-1, keepdims=True)
    raised = jnp.exp(scores - highest)
    probs = raised / jnp.sum(raised, axis=-1, keepdims=True)
    probs_low = probs.astype(jnp.bfloat16)
    attended = jnp.einsum(
        "bphfg,bgphe->bfphe", probs_low, value_rows, preferred_element_type=jnp.float32
    ).astype(jnp.bfloat16)
    return (attended, probs, probs_low)


def attend_back(queries, key_rows, value_rows, probs, probs_low, attended_grad):
    scaling = 1.0 / math.sqrt(queries.shape[-1])
    value_grad = jnp.einsum(
        "bphfg,bfphe->bgphe", probs_low, attended_grad, preferred_element_type=jnp.float32
    ).astype(jnp.bfloat16)
    prob_grad = jnp.einsum(
        "bfphe,bgphe->bphfg", attended_grad, value_rows, preferred_element_type=jnp.float32
    )
    score_grad = probs * (prob_grad - jnp.sum(probs * prob_grad, axis=-1, keepdims=True)) * scaling
    score_low = score_grad.astype(jnp.bfloat16)
    query_grad = jnp.einsum(
        "bphfg,bgphe->bfphe", score_low, key_rows, preferred_element_type=jnp.float32
    ).astype(jnp.bfloat16)
    key_grad = jnp.einsum(
        "bphfg,bfphe->bgphe", score_low, queries, preferred_element_type=jnp.float32
    ).astype(jnp.bfloat16)
    return (query_grad, key_grad, value_grad)


def body(latents, modulation, in_weight, out_weight, up_weight, down_weight, cotangent):
    width = latents.shape[-1]
    local_width = out_weight.shape[0]
    heads_here = local_width // HEAD_DIM
    modulate = modulation[:, :, None, None, :]
    shift_first, scale_first, gate_first = (modulate[:, 0], modulate[:, 1], modulate[:, 2])
    shift_second, scale_second, gate_second = (modulate[:, 3], modulate[:, 4], modulate[:, 5])
    inputs = latents.astype(jnp.float32)
    first_normed, first_inverse = normalize(inputs)
    first_input = (first_normed * (1.0 + scale_first) + shift_first).astype(jnp.bfloat16)
    first_full = gathered_copies(first_input, "tensor", 2)
    in_flat = in_weight.reshape(width, 3 * local_width)
    projected = flat_dot(first_full, in_flat).astype(jnp.bfloat16)
    by_pixel = lax.all_to_all(projected, "seq", split_axis=2, concat_axis=1, tiled=True)
    samples, frames_all, pixel_part = (by_pixel.shape[0], by_pixel.shape[1], by_pixel.shape[2])
    split_parts = by_pixel.reshape(samples, frames_all, pixel_part, 3, heads_here, HEAD_DIM)
    queries, key_rows, value_rows = (
        split_parts[:, :, :, 0],
        split_parts[:, :, :, 1],
        split_parts[:, :, :, 2],
    )
    attended, probs, probs_low = attend(queries, key_rows, value_rows)
    attended_pix = attended.reshape(samples, frames_all, pixel_part, local_width)
    attended_rows = lax.all_to_all(attended_pix, "seq", split_axis=1, concat_axis=2, tiled=True)
    attention = sent_and_summed(
        flat_dot(attended_rows, out_weight).astype(jnp.bfloat16), "tensor", 2
    )
    midway = inputs + gate_first * attention
    second_normed, second_inverse = normalize(midway)
    second_input = (second_normed * (1.0 + scale_second) + shift_second).astype(jnp.bfloat16)
    second_full = gathered_copies(second_input, "tensor", 2)
    hidden = flat_dot(second_full, up_weight)
    activated = gelu_tanh(hidden).astype(jnp.bfloat16)
    feedforward = sent_and_summed(
        flat_dot(activated, down_weight).astype(jnp.bfloat16), "tensor", 2
    )
    result = (midway + gate_second * feedforward).astype(jnp.bfloat16)
    upstream = cotangent.astype(jnp.float32)
    branch_grad = (gate_second * upstream).astype(jnp.bfloat16)
    branch_full = gathered_copies(branch_grad, "tensor", 2)
    down_local = weight_grad(activated, branch_full)
    activated_grad = flat_dot_t(branch_full, down_weight)
    hidden_grad = jax.vjp(gelu_tanh, hidden)[1](activated_grad)[0].astype(jnp.bfloat16)
    up_local = weight_grad(second_full, hidden_grad)
    second_grad = sent_and_summed(
        flat_dot_t(hidden_grad, up_weight).astype(jnp.bfloat16), "tensor", 2
    )
    midway_grad = upstream + norm_back(
        second_normed, second_inverse, second_grad * (1.0 + scale_second)
    )
    attention_grad = (gate_first * midway_grad).astype(jnp.bfloat16)
    attention_full = gathered_copies(attention_grad, "tensor", 2)
    out_local = weight_grad(attended_rows, attention_full)
    attended_grad = flat_dot_t(attention_full, out_weight).astype(jnp.bfloat16)
    grad_pixels = lax.all_to_all(attended_grad, "seq", split_axis=2, concat_axis=1, tiled=True)
    grad_pixels = grad_pixels.reshape(samples, frames_all, pixel_part, heads_here, HEAD_DIM)
    query_grad, key_grad, value_grad = attend_back(
        queries, key_rows, value_rows, probs, probs_low, grad_pixels
    )
    stacked_grad = jnp.stack([query_grad, key_grad, value_grad], axis=3).reshape(
        samples, frames_all, pixel_part, 3 * local_width
    )
    projected_grad = lax.all_to_all(stacked_grad, "seq", split_axis=1, concat_axis=2, tiled=True)
    in_local = weight_grad(first_full, projected_grad).reshape(width, 3, local_width)
    first_grad = sent_and_summed(
        flat_dot_t(projected_grad, in_flat).astype(jnp.bfloat16), "tensor", 2
    )
    latents_grad = (
        midway_grad + norm_back(first_normed, first_inverse, first_grad * (1.0 + scale_first))
    ).astype(jnp.bfloat16)
    down_local, out_local = tuple(
        (
            part.astype(jnp.float32)
            for part in in_one_piece(
                (down_local.astype(jnp.bfloat16), out_local.astype(jnp.bfloat16)),
                ("dp", "seq"),
                1,
                0,
            )
        )
    )
    up_local, in_local = tuple(
        (
            part.astype(jnp.float32)
            for part in sum_packed(
                (up_local.astype(jnp.bfloat16), in_local.astype(jnp.bfloat16)),
                ("dp", "seq"),
                (0, 0),
            )
        )
    )
    return (
        result,
        latents_grad,
        in_local.astype(jnp.bfloat16),
        out_local.astype(jnp.bfloat16),
        up_local.astype(jnp.bfloat16),
        down_local.astype(jnp.bfloat16),
    )


def solution(mesh):
    placed = (
        P("dp", "seq", "tensor", None),
        P("dp", None, None),
        P(None, None, "tensor"),
        P("tensor", None),
        P(None, "tensor"),
        P("tensor", None),
        P("dp", "seq", "tensor", None),
    )
    return jax.shard_map(
        body,
        mesh=mesh,
        in_specs=placed,
        out_specs=(
            P("dp", "seq", "tensor", None),
            P("dp", "seq", "tensor", None),
            P(("dp", "seq"), None, "tensor"),
            P("tensor", ("dp", "seq")),
            P(("dp", "seq"), "tensor"),
            P("tensor", ("dp", "seq")),
        ),
        check_vma=False,
    )
```

profile of v0, /device:TPU:0, one launch (start us, length us, event | category | flops | bytes accessed | tf_op | source)
XLA Modules:
  0.0 403.6 jit_solution(9402229805422721903)
XLA Ops:
  12.5 21.0 %all_to_all.100 = bf16[4,1,2,64,1152]{4,3,2,1,0:T(8,128)(2,1)S(1)} all-to-all(bf16[4,1,2,64,1152]{4,3,2,1,0:T(8,128)(2,1)S(1)} %broadcast_in_dim.20), channel_id=1, replica_groups=mesh['dp'=4,'seq'=8,'tensor'=4] {'tensor'}, dimensions={0} | all-to-all | bytes 2359296 | tf_op jit(solution)/shard_map/all_to_all | solution.py:16
  36.0 2.3 copy.79
  38.2 22.1 %all_to_all.101 = bf16[1,2,256,864]{3,1,0,2:T(2,128)(2,1)S(1)} all-to-all(bf16[1,2,256,864]{3,1,0,2:T(2,128)(2,1)} %copy.79), channel_id=1, replica_groups=mesh['dp'=4,'seq'=8,'tensor'=4] {'seq'}, dimensions={2} | all-to-all | bytes 1769472 | tf_op jit(solution)/shard_map/all_to_all | solution.py:156
  61.4 4.1 %reshape.387 = bf16[1,16,32,3,4,72]{5,4,3,2,1,0:T(4,128)(2,1)} reshape(bf16[1,8,2,32,864]{4,3,2,1,0:T(8,128)(2,1)} %copy.81) | data formatting | bytes 1769472 | tf_op jit(solution)/shard_map/reshape | solution.py:158
  65.6 3.4 fusion.69
  69.0 3.4 fusion.70
  75.5 12.7 %all_to_all.102 = bf16[1,16,32,288]{3,2,0,1:T(8,128)(2,1)S(1)} all-to-all(bf16[1,16,32,288]{3,2,0,1:T(8,128)(2,1)} %bitcast.194), channel_id=1, replica_groups=mesh['dp'=4,'seq'=8,'tensor'=4] {'seq'}, dimensions={1} | all-to-all | bytes 589824 | tf_op jit(solution)/shard_map/all_to_all | solution.py:166
  88.2 2.0 convolution_convert_fusion.6
  91.4 4.3 %all-to-all-start.3 = ((bf16[4,1,2,64,1152]{4,3,2,1,0:T(8,128)(2,1)}), bf16[4,1,2,64,1152]{4,3,2,1,0:T(8,128)(2,1)}, u32[]{:S(2)}, u32[]{:S(2)}) async-start(bf16[4,1,2,64,1152]{4,3,2,1,0:T(8,128)(2,1)} %bitcast.184), calls=%async_computation.3 | async-start | bytes 2359296 | tf_op jit(solution)/shard_map/all_to_all | solution.py:39
  95.8 12.7 %all-to-all-done.3 = bf16[4,1,2,64,1152]{4,3,2,1,0:T(8,128)(2,1)} async-done(((bf16[4,1,2,64,1152]{4,3,2,1,0:T(8,128)(2,1)}), bf16[4,1,2,64,1152]{4,3,2,1,0:T(8,128)(2,1)}, u32[]{:S(2)}, u32[]{:S(2)}) %all-to-all-start.3) | async-done | bytes 1179680 | tf_op jit(solution)/shard_map/all_to_all | solution.py:39
  109.6 4.4 %all-to-all-start.6 = ((bf16[4,1,2,64,1152]{4,3,2,1,0:T(8,128)(2,1)}), bf16[4,1,2,64,1152]{4,3,2,1,0:T(8,128)(2,1)}, u32[]{:S(2)}, u32[]{:S(2)}) async-start(bf16[4,1,2,64,1152]{4,3,2,1,0:T(8,128)(2,1)} %broadcast_in_dim.24), calls=%async_computation.6 | async-start | bytes 2359296 | tf_op jit(solution)/shard_map/all_to_all | solution.py:16
  118.1 7.6 %all-to-all-done.6 = bf16[4,1,2,64,1152]{4,3,2,1,0:T(8,128)(2,1)} async-done(((bf16[4,1,2,64,1152]{4,3,2,1,0:T(8,128)(2,1)}), bf16[4,1,2,64,1152]{4,3,2,1,0:T(8,128)(2,1)}, u32[]{:S(2)}, u32[]{:S(2)}) %all-to-all-start.6) | async-done | bytes 1179680 | tf_op jit(solution)/shard_map/all_to_all | solution.py:16
  125.7 2.1 broadcast_in_dim.22
  127.8 4.4 %all-to-all-start.4 = ((bf16[4,1,2,64,1152]{4,3,2,1,0:T(8,128)(2,1)}), bf16[4,1,2,64,1152]{4,3,2,1,0:T(8,128)(2,1)}, u32[]{:S(2)}, u32[]{:S(2)}) async-start(bf16[4,1,2,64,1152]{4,3,2,1,0:T(8,128)(2,1)} %broadcast_in_dim.22), calls=%async_computation.4 | async-start | bytes 2359296 | tf_op jit(solution)/shard_map/all_to_all | solution.py:16
  134.7 5.0 %fusion.71 = f32[512,1152]{1,0:T(8,128)} fusion(bf16[512,1152]{1,0:T(8,128)(2,1)S(1)} %bitcast.199, bf16[1152,1152]{1,0:T(8,128)(2,1)} %param.12), kind=kOutput, calls=%fused_computation.134 | convolution fusion | flops 1358954496 | bytes 6193152 | tf_op jit(solution)/shard_map/dot_general | solution.py:90
  139.7 4.0 all-to-all-done.4
  145.7 3.8 fusion.13
  151.6 14.0 %all_to_all.103 = bf16[4,1,2,64,1152]{4,3,2,1,0:T(8,128)(2,1)S(1)} all-to-all(bf16[4,1,2,64,1152]{4,3,2,1,0:T(8,128)(2,1)S(1)} %bitcast.186), channel_id=1, replica_groups=mesh['dp'=4,'seq'=8,'tensor'=4] {'tensor'}, dimensions={0} | all-to-all | bytes 2359296 | tf_op jit(solution)/shard_map/all_to_all | solution.py:39
  168.1 4.3 %all-to-all-start.8 = ((bf16[4,1,2,64,1152]{4,3,2,1,0:T(8,128)(2,1)}), bf16[4,1,2,64,1152]{4,3,2,1,0:T(8,128)(2,1)}, u32[]{:S(2)}, u32[]{:S(2)}) async-start(bf16[4,1,2,64,1152]{4,3,2,1,0:T(8,128)(2,1)} %broadcast_in_dim.26), calls=%async_computation.8 | async-start | bytes 2359296 | tf_op jit(solution)/shard_map/all_to_all | solution.py:16
  172.4 4.5 %convolution_convert_fusion.1 = bf16[1152,1152]{1,0:T(8,128)(2,1)} fusion(bf16[512,1152]{1,0:T(8,128)(2,1)S(1)} %bitcast.202, bf16[512,1152]{1,0:T(8,128)(2,1)} %copy-done.42), kind=kOutput, calls=%fused_computation.6 | convolution fusion | flops 1360281600 | bytes 5013504 | tf_op jit(solution)/shard_map/dot_general | solution.py:100
  176.9 5.4 %reshape_reshape.24 = bf16[32,41472]{1,0:T(8,128)(2,1)S(1)} reshape(bf16[1152,1152]{1,0:T(8,128)(2,1)} %convolution_convert_fusion.1) | data formatting | bytes 5308416 | tf_op jit(solution)/shard_map/reshape;reshape | solution.py:53
  187.8 1.9 copy.96
  189.7 4.3 %all-to-all-start.9 = ((bf16[1,2,256,288]{3,1,0,2:T(2,128)(2,1)}), bf16[1,2,256,288]{3,1,0,2:T(2,128)(2,1)}, u32[]{:S(2)}, u32[]{:S(2)}) async-start(bf16[1,2,256,288]{3,1,0,2:T(2,128)(2,1)} %copy.96), calls=%async_computation.9 | async-start | bytes 786432 | tf_op jit(solution)/shard_map/all_to_all | solution.py:197
  194.1 4.9 %convolution_convert_fusion = bf16[1152,1152]{1,0:T(8,128)(2,1)} fusion(bf16[512,1152]{1,0:T(8,128)(2,1)} %get-tuple-element.41, bf16[512,1152]{1,0:T(8,128)(2,1)} %bitcast.200), kind=kOutput, calls=%fused_computation.5 | convolution fusion | flops 1360281600 | bytes 5013504 | tf_op jit(solution)/shard_map/dot_general | solution.py:100
  198.9 3.9 all-to-all-done.9
  204.7 2.1 reshape.395
  206.8 2.7 fusion.24
  211.2 3.9 fusion.23
  215.1 4.1 %fusion.22 = bf16[1,16,32,1,4,72]{5,1,4,2,3,0:T(8,128)(2,1)} fusion(f32[32,4,16,16]{2,3,1,0:T(8,128)} %fusion.51, bf16[1,16,32,1,4,72]{5,4,3,2,1,0:T(4,128)(2,1)} %get-tuple-element.42, f32[32,4,16,16]{2,3,1,0:T(8,128)} %get-tuple-element.48, f32[32,4,16]{2,1,0:T(4,128)} %copy-done.45), kind=kOutput, calls=%fused_computation.46 | convolution fusion | flops 5097487 | bytes 860160 | tf_op jit(solution)/shard_map/bphfg,bgphe->bfphe/dot_general | solution.py:134
  222.8 3.6 reshape.396
  226.4 4.2 %all-to-all-start.10 = ((bf16[1,16,32,864]{3,2,0,1:T(8,128)(2,1)}), bf16[1,16,32,864]{3,2,0,1:T(8,128)(2,1)}, u32[]{:S(2)}, u32[]{:S(2)}) async-start(bf16[1,16,32,864]{3,2,0,1:T(8,128)(2,1)} %bitcast.191), calls=%async_computation.10 | async-start | bytes 1835008 | tf_op jit(solution)/shard_map/all_to_all | solution.py:205
  230.9 2.0 convolution_convert_fusion.7
  232.9 3.7 pad_maximum_fusion
  236.6 5.5 %all-to-all-done.10 = bf16[1,16,32,864]{3,2,0,1:T(8,128)(2,1)} async-done(((bf16[1,16,32,864]{3,2,0,1:T(8,128)(2,1)}), bf16[1,16,32,864]{3,2,0,1:T(8,128)(2,1)}, u32[]{:S(2)}, u32[]{:S(2)}) %all-to-all-start.10) | async-done | bytes 884768 | tf_op jit(solution)/shard_map/all_to_all | solution.py:205
  242.1 2.2 copy.104
  244.3 2.2 copy.109
  246.5 4.1 %convolution_convert_fusion.2 = bf16[1152,3,288]{0,2,1:T(8,128)(2,1)} fusion(bf16[512,1152,1]{1,0,2:T(8,128)(2,1)} %bitcast.198, bf16[3,288,512]{2,1,0:T(8,128)(2,1)} %bitcast.206), kind=kOutput, calls=%fused_computation.8 | convolution fusion | flops 1020211200 | bytes 4055040 | tf_op jit(solution)/shard_map/dot_general | solution.py:100
  250.6 7.2 %copy.110 = bf16[1152,3,288]{2,1,0:T(4,128)(2,1)} copy(bf16[1152,3,288]{0,2,1:T(8,128)(2,1)} %convolution_convert_fusion.2) | data formatting | bytes 3981312 | tf_op jit(solution)/shard_map/convert_element_type | solution.py:228
  257.8 5.4 %reshape_reshape.26 = bf16[32,31104]{1,0:T(8,128)(2,1)} reshape(bf16[1152,3,288]{2,1,0:T(4,128)(2,1)} %copy.110) | data formatting | bytes 3981312 | tf_op jit(solution)/shard_map/reshape;reshape | solution.py:53
  263.2 3.5 fusion.4
  266.7 6.0 %reshape.399 = bf16[18176,128]{1,0:T(8,128)(2,1)} reshape(bf16[32,72704]{1,0:T(8,128)(2,1)} %fusion.4) | data formatting | bytes 9306112 | tf_op jit(solution)/shard_map/reshape | solution.py:55
  273.9 3.6 convolution_convert_fusion.5
  278.7 3.5 all-to-all-start.5
  282.2 3.1 convolution_convert_fusion.3
  286.4 12.8 %all-to-all-done.5 = bf16[4,1,2,64,1152]{4,3,2,1,0:T(8,128)(2,1)S(1)} async-done(((bf16[4,1,2,64,1152]{4,3,2,1,0:T(8,128)(2,1)}), bf16[4,1,2,64,1152]{4,3,2,1,0:T(8,128)(2,1)S(1)}, u32[]{:S(2)}, u32[]{:S(2)}) %all-to-all-start.5) | async-done | bytes 1179680 | tf_op jit(solution)/shard_map/all_to_all | solution.py:39
  299.2 3.5 all-to-all-start.11
  305.7 8.6 %all-to-all-done.11 = bf16[4,1,2,64,1152]{4,3,2,1,0:T(8,128)(2,1)S(1)} async-done(((bf16[4,1,2,64,1152]{4,3,2,1,0:T(8,128)(2,1)}), bf16[4,1,2,64,1152]{4,3,2,1,0:T(8,128)(2,1)S(1)}, u32[]{:S(2)}, u32[]{:S(2)}) %all-to-all-start.11) | async-done | bytes 1179680 | tf_op jit(solution)/shard_map/all_to_all | solution.py:39
  316.9 72.6 %all-reduce.6.cloned.1.call-done = (bf16[18176,128]{1,0:T(8,128)(2,1)}, bf16[1440,1152]{1,0:T(8,128)(2,1)}) async-done(((bf16[18176,128]{1,0:T(8,128)(2,1)}, bf16[1440,1152]{1,0:T(8,128)(2,1)}), (bf16[18176,128]{1,0:T(8,128)(2,1)}, bf16[1440,1152]{1,0:T(8,128)(2,1)})) %all-reduce.6.cloned.1.call-update) | async-done | bytes 7970832
  (155 shorter events, 54.9 us)
Async XLA Ops:
  7.2 138.1 %copy-start = (bf16[1152,1152]{1,0:T(8,128)(2,1)S(1)}, bf16[1152,1152]{1,0:T(8,128)(2,1)}, u32[]{:S(2)}) copy-start(bf16[1152,1152]{1,0:T(8,128)(2,1)} %param.11) | copy-start | bytes 7962628
  9.9 23.6 %copy-start.30 = (f32[2,64]{1,0:T(2,128)}, f32[2,64]{1,0:T(2,128)S(1)}, u32[]{:S(2)}) copy-start(f32[2,64]{1,0:T(2,128)S(1)} %broadcast_multiply_fusion.5) | copy-start | bytes 1540
  11.1 22.4 %copy-start.33 = (f32[2,64]{1,0:T(2,128)}, f32[2,64]{1,0:T(2,128)S(1)}, u32[]{:S(2)}) copy-start(f32[2,64]{1,0:T(2,128)S(1)} %add_rsqrt_fusion.1) | copy-start | bytes 1540
  12.5 22.2 %copy-start.40 = (bf16[1152,3,288]{0,2,1:T(8,128)(2,1)S(1)}, bf16[1152,3,288]{0,2,1:T(8,128)(2,1)}, u32[]{:S(2)}) copy-start(bf16[1152,3,288]{0,2,1:T(8,128)(2,1)} %param.9) | copy-start | bytes 5971972
  69.0 3.4 copy-start.13
  72.4 1.8 copy-start.45
  88.2 3.2 copy-start.7
  90.2 5.4 %copy-start.8 = (bf16[1,2,64,1152]{3,2,1,0:T(8,128)(2,1)S(1)}, bf16[1,2,64,1152]{3,2,1,0:T(8,128)(2,1)}, u32[]{:S(2)}) copy-start(bf16[1,2,64,1152]{3,2,1,0:T(8,128)(2,1)} %param.13) | copy-start | bytes 884740
  90.3 5.4 %copy-start.20 = (f32[1152]{0:T(1024)S(1)}, f32[1152]{0:T(1024)}, u32[]{:S(2)}) copy-start(f32[1152]{0:T(1024)} %get-tuple-element.30) | copy-start | bytes 13828
  91.4 17.1 %all-to-all-start.3 = ((bf16[4,1,2,64,1152]{4,3,2,1,0:T(8,128)(2,1)}), bf16[4,1,2,64,1152]{4,3,2,1,0:T(8,128)(2,1)}, u32[]{:S(2)}, u32[]{:S(2)}) async-start(bf16[4,1,2,64,1152]{4,3,2,1,0:T(8,128)(2,1)} %bitcast.184), calls=%async_computation.3 | async-start | bytes 2359296 | tf_op jit(solution)/shard_map/all_to_all | solution.py:39
  109.6 5.9 %copy-start.4 = (bf16[1,2,64,1152]{3,2,1,0:T(8,128)(2,1)S(1)}, bf16[1,2,64,1152]{3,2,1,0:T(8,128)(2,1)}, u32[]{:S(2)}) copy-start(bf16[1,2,64,1152]{3,2,1,0:T(8,128)(2,1)} %param.7) | copy-start | bytes 884740
  109.6 16.1 %all-to-all-start.6 = ((bf16[4,1,2,64,1152]{4,3,2,1,0:T(8,128)(2,1)}), bf16[4,1,2,64,1152]{4,3,2,1,0:T(8,128)(2,1)}, u32[]{:S(2)}, u32[]{:S(2)}) async-start(bf16[4,1,2,64,1152]{4,3,2,1,0:T(8,128)(2,1)} %broadcast_in_dim.24), calls=%async_computation.6 | async-start | bytes 2359296 | tf_op jit(solution)/shard_map/all_to_all | solution.py:16
  114.0 3.2 copy-start.26
  127.8 15.9 %all-to-all-start.4 = ((bf16[4,1,2,64,1152]{4,3,2,1,0:T(8,128)(2,1)}), bf16[4,1,2,64,1152]{4,3,2,1,0:T(8,128)(2,1)}, u32[]{:S(2)}, u32[]{:S(2)}) async-start(bf16[4,1,2,64,1152]{4,3,2,1,0:T(8,128)(2,1)} %broadcast_in_dim.22), calls=%async_computation.4 | async-start | bytes 2359296 | tf_op jit(solution)/shard_map/all_to_all | solution.py:16
  143.7 2.0 copy-start.44
  145.2 4.3 %copy-start.17 = (bf16[4,1,2,64,1152]{4,3,0,2,1:T(8,128)(2,1)}, bf16[4,1,2,64,1152]{4,3,0,2,1:T(8,128)(2,1)S(1)}, u32[]{:S(2)}) copy-start(bf16[4,1,2,64,1152]{4,3,0,2,1:T(8,128)(2,1)S(1)} %copy.91) | copy-start | bytes 3538948
  149.5 1.9 copy-start.42
  151.6 14.2 %copy-start.24 = (f32[2,64]{1,0:T(2,128)S(1)}, f32[2,64]{1,0:T(2,128)}, u32[]{:S(2)}) copy-start(f32[2,64]{1,0:T(2,128)} %copy-done.23) | copy-start | bytes 1540
  151.6 14.2 %copy-start.28 = (f32[2,64]{1,0:T(2,128)S(1)}, f32[2,64]{1,0:T(2,128)}, u32[]{:S(2)}) copy-start(f32[2,64]{1,0:T(2,128)} %copy-done.27) | copy-start | bytes 1540
  165.8 2.3 copy-start.2
  166.2 2.0 copy-start.36
  166.2 2.0 copy-start.38
  167.0 5.4 %copy-start.18 = (bf16[4,1,2,64,1152]{4,3,0,2,1:T(8,128)(2,1)S(1)}, bf16[4,1,2,64,1152]{4,3,0,2,1:T(8,128)(2,1)}, u32[]{:S(2)}) copy-start(bf16[4,1,2,64,1152]{4,3,0,2,1:T(8,128)(2,1)} %copy-done.17) | copy-start | bytes 3538948
  168.1 15.9 %all-to-all-start.8 = ((bf16[4,1,2,64,1152]{4,3,2,1,0:T(8,128)(2,1)}), bf16[4,1,2,64,1152]{4,3,2,1,0:T(8,128)(2,1)}, u32[]{:S(2)}, u32[]{:S(2)}) async-start(bf16[4,1,2,64,1152]{4,3,2,1,0:T(8,128)(2,1)} %broadcast_in_dim.26), calls=%async_computation.8 | async-start | bytes 2359296 | tf_op jit(solution)/shard_map/all_to_all | solution.py:16
  184.1 2.5 copy-start.19
  189.7 13.1 %all-to-all-start.9 = ((bf16[1,2,256,288]{3,1,0,2:T(2,128)(2,1)}), bf16[1,2,256,288]{3,1,0,2:T(2,128)(2,1)}, u32[]{:S(2)}, u32[]{:S(2)}) async-start(bf16[1,2,256,288]{3,1,0,2:T(2,128)(2,1)} %copy.96), calls=%async_computation.9 | async-start | bytes 786432 | tf_op jit(solution)/shard_map/all_to_all | solution.py:197
  206.8 2.7 copy-start.12
  206.8 2.7 copy-start.14
  226.4 15.7 %all-to-all-start.10 = ((bf16[1,16,32,864]{3,2,0,1:T(8,128)(2,1)}), bf16[1,16,32,864]{3,2,0,1:T(8,128)(2,1)}, u32[]{:S(2)}, u32[]{:S(2)}) async-start(bf16[1,16,32,864]{3,2,0,1:T(8,128)(2,1)} %bitcast.191), calls=%async_computation.10 | async-start | bytes 1835008 | tf_op jit(solution)/shard_map/all_to_all | solution.py:205
  230.6 158.9 %all-reduce.6.cloned.1.call-start = ((), (), s32[]{:S(2)}) async-start(), calls=%async_computation.12 | async-start | bytes 15941632
  272.7 1.3 copy-start.41
  277.5 4.7 %copy-start.6 = (bf16[1,2,8,32,864]{4,3,2,1,0:T(8,128)(2,1)S(1)}, bf16[1,2,8,32,864]{4,3,2,1,0:T(8,128)(2,1)}, u32[]{:S(2)}) copy-start(bf16[1,2,8,32,864]{4,3,2,1,0:T(8,128)(2,1)} %copy.104) | copy-start | bytes 2654212
  278.7 20.6 %all-to-all-start.5 = ((bf16[4,1,2,64,1152]{4,3,2,1,0:T(8,128)(2,1)}), bf16[4,1,2,64,1152]{4,3,2,1,0:T(8,128)(2,1)S(1)}, u32[]{:S(2)}, u32[]{:S(2)}) async-start(bf16[4,1,2,64,1152]{4,3,2,1,0:T(8,128)(2,1)} %bitcast.180), calls=%async_computation.5 | async-start | bytes 2359296 | tf_op jit(solution)/shard_map/all_to_all | solution.py:39
  285.3 17.5 %copy-start.43 = (u32[128]{0:T(128)S(1)}, u32[128]{0:T(128)}, u32[]{:S(2)}) copy-start(u32[128]{0:T(128)} %constant.41) | copy-start | bytes 1540
  299.2 15.1 %all-to-all-start.11 = ((bf16[4,1,2,64,1152]{4,3,2,1,0:T(8,128)(2,1)}), bf16[4,1,2,64,1152]{4,3,2,1,0:T(8,128)(2,1)S(1)}, u32[]{:S(2)}, u32[]{:S(2)}) async-start(bf16[4,1,2,64,1152]{4,3,2,1,0:T(8,128)(2,1)} %bitcast.178), calls=%async_computation.11 | async-start | bytes 2359296 | tf_op jit(solution)/shard_map/all_to_all | solution.py:39
  304.7 10.0 %copy-start.31 = (f32[2,64]{1,0:T(2,128)S(1)}, f32[2,64]{1,0:T(2,128)}, u32[]{:S(2)}) copy-start(f32[2,64]{1,0:T(2,128)} %copy-done.30) | copy-start | bytes 1540
  304.7 10.0 %copy-start.34 = (f32[2,64]{1,0:T(2,128)S(1)}, f32[2,64]{1,0:T(2,128)}, u32[]{:S(2)}) copy-start(f32[2,64]{1,0:T(2,128)} %copy-done.33) | copy-start | bytes 1540
  314.3 1.1 copy-start.3
  314.3 1.1 copy-start.10
  314.3 1.3 copy-start.11
  314.3 1.3 copy-start.21
  314.3 1.3 copy-start.25
  314.3 1.3 copy-start.29
  314.4 1.3 copy-start.32
  314.4 1.3 copy-start.35
  314.4 1.3 copy-start.37
  314.4 1.3 copy-start.39
  315.0 81.8 %copy-start.1 = (bf16[1152,1152]{1,0:T(8,128)(2,1)S(1)}, bf16[1152,1152]{1,0:T(8,128)(2,1)}, u32[]{:S(2)}) copy-start(bf16[1152,1152]{1,0:T(8,128)(2,1)} %param.11) | copy-start | bytes 7962628
  (7 other events, 6.1 us)
Sparse Core Ops, SparseCore 0:
  272.8 116.7 all-reduce.5
where the time goes:
time: 407 us; the launch traced here: 404 us
  waiting for transfers between devices  129 us (32%)
  local copies, waits for them, and re-layouts  78.8 us (19%)
  blocking collectives  69.8 us (17%)
  matrix products  55 us (14%)
  starting transfers between devices  33.3 us (8%)
  other arithmetic  21.2 us (5%)
  between operations  16 us (4%)
    unnamed x2, waiting for transfers between devices  72.7 us
    all_to_all x3, waiting for transfers between devices, sent_and_summed(): lax.all_to_all(pieces, axis, split_axis=0, concat_axis=0, tiled=True)  34.1 us
    all_to_all x1, blocking collectives, body(): lax.all_to_all(projected, 'seq', split_axis=2, concat_axis=1, tiled=True)  22.1 us
    all_to_all x1, blocking collectives, from_everyone(): lax.all_to_all(jnp.broadcast_to(array[None], (size, *array.shape)), axis,...  21 us
    dot_general x4, matrix products, weight_grad(): lax.dot_general(left.reshape(-1, left.shape[-1]), right.reshape(-1, right...  15.5 us
    all_to_all x1, blocking collectives, sent_and_summed(): lax.all_to_all(pieces, axis, split_axis=0, concat_axis=0, tiled=True)  14 us
    all_to_all x3, waiting for transfers between devices, from_everyone(): lax.all_to_all(jnp.broadcast_to(array[None], (size, *array.shape)), axis,...  13.3 us
    all_to_all x3, starting transfers between devices, from_everyone(): lax.all_to_all(jnp.broadcast_to(array[None], (size, *array.shape)), axis,...  13.1 us
  transfers between devices with their start and end apart: 9, of which 9 were waited for; matrix products, arithmetic and copies ran while one was open for 11% of the time, Pallas kernels for 0%

commit v1 on v0

v1 whole, which is shorter than its diff:
```python
import math

import jax
import jax.numpy as jnp
from jax import lax
from jax.experimental import pallas as pl
from jax.experimental.pallas import tpu as pltpu
from jax.sharding import PartitionSpec as P

HEAD_DIM = 72
HEADS = 4
D = 1152
W = 288
WP = 384
SCALE = 1.0 / math.sqrt(HEAD_DIM)
EPS = 1e-6
MESH = pl.DeviceIdType.MESH
F32 = jnp.float32
BF16 = jnp.bfloat16
GELU_C = math.sqrt(2.0 / math.pi)

NN = (((1,), (0,)), ((), ()))
NT = (((1,), (1,)), ((), ()))
TN = (((0,), (0,)), ((), ()))


def rem(a, b):
    return lax.rem(a, b)


def div(a, b):
    return lax.div(a, b)


def dot(a, b, dims):
    return lax.dot_general(a, b, dims, preferred_element_type=F32)


def norm(rows):
    center = jnp.mean(rows, axis=-1, keepdims=True)
    centred = rows - center
    spread = jnp.mean(centred * centred, axis=-1, keepdims=True)
    inverse = lax.rsqrt(spread + EPS)
    return centred * inverse, inverse


def norm_back(normed, inverse, up):
    mean_grad = jnp.mean(up, axis=-1, keepdims=True)
    mean_cross = jnp.mean(up * normed, axis=-1, keepdims=True)
    return (up - mean_grad - normed * mean_cross) * inverse


JOBS = (("u", 1152, True), ("d", 1152, False), ("i", 768, True), ("v", 768, False))


def scratch_spec():
    vm = lambda *s, t=BF16: pltpu.VMEM(s, t)
    dma = lambda *s: pltpu.SemaphoreType.DMA(s)
    spec = {
        "xs": vm(8, 2, 8, D), "cs": vm(8, 2, 8, D),
        "win": vm(3, WP, D), "wout": vm(WP, D), "wup": vm(D, D), "wdown": vm(D, D),
        "f": vm(4, 128, D), "s": vm(4, 128, D), "g": vm(4, 128, D), "a": vm(4, 128, D),
        "p2": vm(4, 128, D), "p5": vm(4, 128, D), "p7": vm(4, 128, D), "p8": vm(4, 128, D),
        "r2": vm(4, 128, D), "r5": vm(4, 128, D), "r7": vm(4, 128, D), "r8": vm(4, 128, D),
        "qkv": vm(4, 128, 3 * WP), "probs": vm(4, 512, 128, t=F32), "att": vm(4, 128, WP),
        "act": vm(4, 128, D), "hg": vm(4, 128, D), "dqkv": vm(4, 128, 3 * WP),
        "mid": vm(128, D, t=F32), "mg": vm(128, D, t=F32),
        "ro": vm(8, 2, 8, D), "lo": vm(8, 2, 8, D), "rl": vm(2, 8, 8, D), "ll": vm(2, 8, 8, D),
        "wsem": dma(6),
        "ys": dma(8, 4), "yr": dma(8, 4),
        "ss": dma(4, 8), "sr": dma(4, 8),
        "osem": dma(2),
        "js": dma(4, 7), "jr": dma(4, 7),
    }
    for name, n, x_first in JOBS:
        spec["G" + name] = vm(2, 2, 4, 9, 8, n)
        spec["A" + name] = vm(2, 4, 9, 8, n)
        if x_first:
            spec["B" + name] = vm(4, 2, 9, 8, n)
            spec["H" + name] = vm(2, 9, 8, n)
        else:
            spec["B" + name] = vm(4, 4, 5, 8, n)
            spec["H" + name] = vm(4, 5, 8, n)
        spec["C" + name] = vm(4, 5, 8, n)
    return spec


SPEC = scratch_spec()


def kernel(lat, cot, mod, in_w, out_w, up_w, down_w, res, lgr, gu, gd, gi, gv, *scratch):
    r = dict(zip(SPEC, scratch))
    dp, seq, me = lax.axis_index("dp"), lax.axis_index("seq"), lax.axis_index("tensor")
    core, z_lo = rem(dp, 2), div(dp, 2)
    x, z_hi = div(seq, 2), rem(seq, 2)
    z = z_hi * 2 + z_lo

    def remote(src, dst, send, recv, where):
        return pltpu.make_async_remote_copy(src_ref=src, dst_ref=dst, send_sem=send, recv_sem=recv, device_id=where, device_id_type=MESH)

    def local(src, dst, sem):
        return pltpu.make_async_copy(src, dst, sem)

    def seq_peer(k):
        return (dp, rem(seq + k, 8), me)

    def y_peer(k):
        return (dp, seq, rem(me + k, 4))

    def core_peer():
        return (dp + 1 - 2 * core, seq, me)

    def x_peer(k):
        return (dp, rem(x + k, 4) * 2 + z_hi, me)

    def z_peer(k):
        other = rem(z + k, 4)
        return (rem(other, 2) * 2 + core, x * 2 + div(other, 2), me)

    weights = [local(in_w.at[j], r["win"].at[j, pl.ds(0, W)], r["wsem"].at[j]) for j in range(3)]
    weights += [
        local(out_w, r["wout"].at[pl.ds(0, W)], r["wsem"].at[3]),
        local(up_w, r["wup"], r["wsem"].at[4]),
        local(down_w, r["wdown"], r["wsem"].at[5]),
    ]

    barrier = pltpu.get_barrier_semaphore()
    peers = [seq_peer(k) for k in range(1, 8)] + [y_peer(k) for k in range(1, 4)] + [core_peer()]
    peers += [z_peer(1), z_peer(3)]
    for where in peers:
        pl.semaphore_signal(barrier, inc=1, device_id=where, device_id_type=MESH)
    pl.semaphore_wait(barrier, len(peers))

    sends = []

    def exchange_in(row, src, dst):
        for k in range(1, 8):
            to = rem(seq + k, 8)
            c = remote(src.at[:, to], dst.at[seq], r["ss"].at[row, k], r["sr"].at[row, k], seq_peer(k))
            c.start()
            sends.append(c)
        c = local(src.at[:, seq], dst.at[seq], r["sr"].at[row, 0])
        c.start()

    def exchange_in_wait(row, src, dst):
        local(src.at[:, seq], dst.at[seq], r["sr"].at[row, 0]).wait()
        for k in range(1, 8):
            frm = rem(seq + 8 - k, 8)
            remote(src.at[:, frm], dst.at[frm], r["ss"].at[row, k], r["sr"].at[row, k], seq_peer(k)).wait_recv()

    exchange_in(0, lat, r["xs"])
    exchange_in(1, cot, r["cs"])
    for c in weights:
        c.start()
    for j in range(3):
        r["win"][j, W:] = jnp.zeros((WP - W, D), BF16)
    r["wout"][W:] = jnp.zeros((WP - W, D), BF16)

    def row(i):
        return mod[i : i + 1, :]

    def halves(ref, h):
        return ref[4 * h : 4 * h + 4].astype(F32).reshape(64, D)

    def gather_start(ph, buf):
        for k in (2, 1, 3):
            c = remote(buf.at[me], buf.at[me], r["ys"].at[ph, k], r["yr"].at[ph, k], y_peer(k))
            c.start()
            sends.append(c)

    def gather_wait(ph, buf, k):
        frm = rem(me + 4 - k, 4)
        remote(buf.at[frm], buf.at[frm], r["ys"].at[ph, k], r["yr"].at[ph, k], y_peer(k)).wait_recv()

    def part_send(ph, src, dst, k):
        to = rem(me + k, 4)
        c = remote(src.at[to], dst.at[me], r["ys"].at[ph, k], r["yr"].at[ph, k], y_peer(k))
        c.start()

    def part_send_wait(ph, src, dst):
        for k in range(1, 4):
            remote(src.at[0], dst.at[me], r["ys"].at[ph, k], r["yr"].at[ph, k], y_peer(k)).wait_send()

    def part_wait(ph, src, dst):
        for k in range(1, 4):
            frm = rem(me + 4 - k, 4)
            remote(src.at[frm], dst.at[frm], r["ys"].at[ph, k], r["yr"].at[ph, k], y_peer(k)).wait_recv()

    def part_sum(src, dst, h):
        rows = pl.ds(64 * h, 64)
        total = src[me, rows, :].astype(F32)
        for k in (1, 2, 3):
            total = total + dst[rem(me + k, 4), rows, :].astype(F32)
        return total

    def block_of(i):
        k = jnp.where(i < 2, i, 5 - i)
        return k, rem(me + k, 4)

    def arrival(ph, buf, i):
        for j, k in ((1, 1), (2, 3), (3, 2)):
            @pl.when(i == j)
            def _():
                gather_wait(ph, buf, 4 - k)

    def part_out(ph, src, dst, i):
        for j, k in ((1, 1), (2, 3), (3, 2)):
            @pl.when(i == j)
            def _():
                part_send(ph, src, dst, k)

    lane = lax.broadcasted_iota(jnp.int32, (128, WP), 1)
    head_masks = [(lane >= HEAD_DIM * h) & (lane < HEAD_DIM * (h + 1)) for h in range(HEADS)]
    same_pixel = rem(lax.broadcasted_iota(jnp.int32, (512, 128), 0), 8) == rem(lax.broadcasted_iota(jnp.int32, (512, 128), 1), 8)

    def stacked(v):
        zero = jnp.zeros_like(v)
        return jnp.concatenate([jnp.where(m, v, zero) for m in head_masks], axis=0)

    def side_by_side(v):
        return jnp.concatenate([v[128 * h : 128 * h + 128] for h in range(HEADS)], axis=1)

    exchange_in_wait(0, lat, r["xs"])
    for h in range(2):
        normed, _ = norm(halves(r["xs"], h))
        r["f"][me, 64 * h : 64 * h + 64, :] = (normed * (1.0 + row(1)) + row(0)).astype(BF16)
    gather_start(0, r["f"])
    exchange_in_wait(1, cot, r["cs"])
    for h in range(2):
        r["g"][me, 64 * h : 64 * h + 64, :] = (row(5) * halves(r["cs"], h)).astype(BF16)

    gather_start(1, r["g"])
    for c in weights[:4]:
        c.wait()

    def attend_block(i, carry):
        k, t = block_of(i)
        arrival(0, r["f"], i)

        block = r["f"][t]
        for j in range(3):
            r["qkv"][t, :, j * WP : (j + 1) * WP] = dot(block, r["win"][j], NT).astype(BF16)
        q, kk, v = (r["qkv"][t, :, j * WP : (j + 1) * WP] for j in range(3))
        scores = dot(stacked(q), kk, NT) * SCALE
        scores = jnp.where(same_pixel, scores, -1e30)
        raised = jnp.exp(scores - jnp.max(scores, axis=-1, keepdims=True))
        probs = raised / jnp.sum(raised, axis=-1, keepdims=True)
        r["probs"][t] = probs
        att = dot(side_by_side(probs.astype(BF16)), stacked(v), NN).astype(BF16)
        r["att"][t] = att
        for n in range(3):
            cols = slice(n * 384, n * 384 + 384)
            r["p2"][t, :, cols] = dot(att, r["wout"][:, cols], NN).astype(BF16)
        part_out(2, r["p2"], r["r2"], i)
        return carry

    lax.fori_loop(0, 4, attend_block, 0)
    part_wait(2, r["p2"], r["r2"])

    for h in range(2):
        rows = slice(64 * h, 64 * h + 64)
        midway = halves(r["xs"], h) + row(2) * part_sum(r["p2"], r["r2"], h)
        r["mid"][rows, :] = midway
        normed, _ = norm(midway)
        r["s"][me, rows, :] = (normed * (1.0 + row(4)) + row(3)).astype(BF16)
    gather_start(3, r["s"])

    weights[4].wait()
    weights[5].wait()

    def mlp_block(i, carry):
        k, t = block_of(i)
        arrival(3, r["s"], i)
        arrival(1, r["g"], i)

        def hidden_cols(n, c):
            cols = pl.ds(pl.multiple_of(n * 384, 384), 384)
            v = dot(r["s"][t], r["wup"][:, cols], NN)
            ag = dot(r["g"][t], r["wdown"][cols, :], NT)
            th = jnp.tanh(GELU_C * (v + 0.044715 * (v * v * v)))
            r["act"][t, :, cols] = (0.5 * v * (1.0 + th)).astype(BF16)
            slope = 0.5 * (1.0 + th) + (0.5 * v) * ((1.0 - th * th) * (GELU_C * (1.0 + (3.0 * 0.044715) * (v * v))))
            r["hg"][t, :, cols] = (ag * slope).astype(BF16)
            return c

        lax.fori_loop(0, 3, hidden_cols, 0)

        def grad_cols(n, c):
            cols = pl.ds(pl.multiple_of(n * 384, 384), 384)
            r["p5"][t, :, cols] = dot(r["hg"][t], r["wup"][cols, :], NT).astype(BF16)
            return c

        lax.fori_loop(0, 3, grad_cols, 0)
        part_out(4, r["p5"], r["r5"], i)

        def result_cols(n, c):
            cols = pl.ds(pl.multiple_of(n * 384, 384), 384)
            r["p8"][t, :, cols] = dot(r["act"][t], r["wdown"][:, cols], NN).astype(BF16)
            return c

        lax.fori_loop(0, 3, result_cols, 0)
        return carry

    lax.fori_loop(0, 4, mlp_block, 0)

    def weight_grad(lhs, rhs, width, name, at):
        def rows_step(m, c):
            cols = pl.ds(pl.multiple_of(m * 384, 384), 384)
            left = lhs[:, :, cols].reshape(512, 384)
            right = rhs().reshape(512, width)
            out = dot(left, right, TN).astype(BF16).reshape(48, 8, width)
            for q in range(48 // 3):
                grp = m * 16 + q
                outer = div(grp, 3)
                r["G" + name][div(outer, 8), rem(div(outer, 4), 2), rem(outer, 4), pl.ds(rem(grp, 3) * 3, 3), :, at : at + width] = out[3 * q : 3 * q + 3]
            return c

        lax.fori_loop(0, 3, rows_step, 0)

    def job(index):
        name, n, x_first = JOBS[index]
        return name, n, x_first

    def job_core(index, start):
        name, n, _ = JOBS[index]
        to = 1 - core if start else core
        c = remote(r["G" + name].at[:, 1 - core], r["A" + name], r["js"].at[index, 0], r["jr"].at[index, 0], core_peer())
        if start:
            c.start()
        else:
            c.wait()

    def job_core_sum(index):
        name, n, _ = JOBS[index]

        def step(i, c):
            a, b = div(i, 4), rem(i, 4)
            total = r["A" + name][a, b].astype(F32) + r["G" + name][a, core, b].astype(F32)
            r["A" + name][a, b] = total.astype(BF16)
            return c

        lax.fori_loop(0, 8, step, 0)

    def job_first(index, start):
        name, n, x_first = JOBS[index]
        for k in (2, 1, 3):
            if x_first:
                src = r["A" + name].at[:, rem(x + k, 4)]
                mine, frm, where = x, rem(x + 4 - k, 4), x_peer(k)
            else:
                other = rem(z + k, 4)
                src = r["A" + name].at[rem(other, 2), :, pl.ds(4 * div(other, 2), 5)]
                mine, frm, where = z, rem(z + 4 - k, 4), z_peer(k)
            if start:
                remote(src, r["B" + name].at[mine], r["js"].at[index, k], r["jr"].at[index, k], where).start()
            else:
                remote(src, r["B" + name].at[frm], r["js"].at[index, k], r["jr"].at[index, k], where).wait()

    def job_first_sum(index):
        name, n, x_first = JOBS[index]
        if x_first:
            for a in range(2):
                total = r["A" + name][a, x].astype(F32)
                for k in (1, 2, 3):
                    total = total + r["B" + name][rem(x + k, 4), a].astype(F32)
                r["H" + name][a] = total.astype(BF16)
        else:
            for b in range(4):
                total = r["A" + name][z_lo, b, pl.ds(4 * z_hi, 5)].astype(F32)
                for k in (1, 2, 3):
                    total = total + r["B" + name][rem(z + k, 4), b].astype(F32)
                r["H" + name][b] = total.astype(BF16)

    def job_second(index, start):
        name, n, x_first = JOBS[index]
        for k in (2, 1, 3):
            if x_first:
                other = rem(z + k, 4)
                src = r["H" + name].at[rem(other, 2), pl.ds(4 * div(other, 2), 5)]
                mine, frm, where = z, rem(z + 4 - k, 4), z_peer(k)
            else:
                src = r["H" + name].at[rem(x + k, 4)]
                mine, frm, where = x, rem(x + 4 - k, 4), x_peer(k)
            if start:
                remote(src, r["C" + name].at[mine], r["js"].at[index, 3 + k], r["jr"].at[index, 3 + k], where).start()
            else:
                remote(src, r["C" + name].at[frm], r["js"].at[index, 3 + k], r["jr"].at[index, 3 + k], where).wait()

    def job_second_sum(index, out):
        name, n, x_first = JOBS[index]
        if x_first:
            total = r["H" + name][z_lo, pl.ds(4 * z_hi, 5)].astype(F32)
            at = z
        else:
            total = r["H" + name][x].astype(F32)
            at = x
        for k in (1, 2, 3):
            total = total + r["C" + name][rem(at + k, 4)].astype(F32)
        out[...] = total.astype(BF16)

    weight_grad(r["s"], lambda: r["hg"][...], D, "u", 0)
    job_core(0, True)

    part_wait(4, r["p5"], r["r5"])
    for h in range(2):
        rows = slice(64 * h, 64 * h + 64)
        normed, inverse = norm(r["mid"][rows, :])
        back = norm_back(normed, inverse, part_sum(r["p5"], r["r5"], h) * (1.0 + row(4)))
        mg = halves(r["cs"], h) + back
        r["mg"][rows, :] = mg
        r["a"][me, rows, :] = (row(2) * mg).astype(BF16)
    gather_start(5, r["a"])
    for k in (1, 3, 2):
        part_send(7, r["p8"], r["r8"], k)

    weight_grad(r["g"], lambda: r["act"][...], D, "d", 0)
    job_core(1, True)
    job_core(0, False)
    job_core_sum(0)
    job_first(0, True)

    def attend_back_block(i, carry):
        k, t = block_of(i)
        arrival(5, r["a"], i)
        grad = dot(r["a"][t], r["wout"][...], NT).astype(BF16)
        q, kk, v = (r["qkv"][t, :, j * WP : (j + 1) * WP] for j in range(3))
        qs, gs = stacked(q), stacked(grad)
        probs = r["probs"][t]
        dv = dot(probs.astype(BF16), gs, TN)
        dp_ = dot(gs, v, NT)
        ds = (probs * (dp_ - jnp.sum(probs * dp_, axis=-1, keepdims=True)) * SCALE).astype(BF16)
        dq = dot(side_by_side(ds), stacked(kk), NN)
        dk = dot(ds, qs, TN)
        for j, part in enumerate((dq, dk, dv)):
            r["dqkv"][t, :, j * WP : (j + 1) * WP] = part.astype(BF16)
        for n in range(3):
            cols = slice(n * 384, n * 384 + 384)
            total = dot(r["dqkv"][t, :, 0:WP], r["win"][0, :, cols], NN)
            for j in (1, 2):
                total = total + dot(r["dqkv"][t, :, j * WP : (j + 1) * WP], r["win"][j, :, cols], NN)
            r["p7"][t, :, cols] = total.astype(BF16)
        part_out(6, r["p7"], r["r7"], i)
        return carry

    lax.fori_loop(0, 2, attend_back_block, 0)
    job_core(1, False)
    job_core_sum(1)
    job_first(1, True)
    lax.fori_loop(2, 4, attend_back_block, 0)

    weight_grad(r["f"], lambda: r["dqkv"][:, :, 0:768], 768, "i", 0)
    job_core(2, True)
    weight_grad(r["f"], lambda: r["dqkv"][:, :, 768:1152], 384, "v", 0)
    weight_grad(r["a"], lambda: r["att"][...], 384, "v", 384)
    job_core(3, True)

    def exchange_out(row_, src, dst):
        for k in range(1, 8):
            to = rem(seq + k, 8)
            remote(src.at[to], dst.at[:, seq], r["ss"].at[row_, k], r["sr"].at[row_, k], seq_peer(k)).start()
        local(src.at[seq], dst.at[:, seq], r["sr"].at[row_, 0]).start()

    def exchange_out_wait(row_, src, dst):
        local(src.at[seq], dst.at[:, seq], r["sr"].at[row_, 0]).wait()
        for k in range(1, 8):
            frm = rem(seq + 8 - k, 8)
            remote(src.at[frm], dst.at[:, frm], r["ss"].at[row_, k], r["sr"].at[row_, k], seq_peer(k)).wait()

    part_wait(7, r["p8"], r["r8"])
    for h in range(2):
        rows = slice(64 * h, 64 * h + 64)
        out = r["mid"][rows, :] + row(5) * part_sum(r["p8"], r["r8"], h)
        r["ro"][4 * h : 4 * h + 4] = out.astype(BF16).reshape(4, 2, 8, D)
    exchange_out(2, r["ro"], r["rl"])

    job_first(0, False)
    job_first_sum(0)
    job_second(0, True)

    part_wait(6, r["p7"], r["r7"])
    for h in range(2):
        rows = slice(64 * h, 64 * h + 64)
        normed, inverse = norm(halves(r["xs"], h))
        back = norm_back(normed, inverse, part_sum(r["p7"], r["r7"], h) * (1.0 + row(1)))
        out = r["mg"][rows, :] + back
        r["lo"][4 * h : 4 * h + 4] = out.astype(BF16).reshape(4, 2, 8, D)
    exchange_out(3, r["lo"], r["ll"])

    job_first(1, False)
    job_first_sum(1)
    job_second(1, True)
    for index in (2, 3):
        job_core(index, False)
        job_core_sum(index)
        job_first(index, True)
    job_second(0, False)
    job_second_sum(0, gu)
    job_second(1, False)
    job_second_sum(1, gd)
    exchange_out_wait(2, r["ro"], r["rl"])
    done = [local(r["rl"], res, r["osem"].at[0])]
    done[0].start()
    for index in (2, 3):
        job_first(index, False)
        job_first_sum(index)
        job_second(index, True)
    exchange_out_wait(3, r["lo"], r["ll"])
    done.append(local(r["ll"], lgr, r["osem"].at[1]))
    done[1].start()
    for index, out in ((2, gi), (3, gv)):
        job_second(index, False)
        job_second_sum(index, out)
    for c in sends:
        c.wait_send()
    for ph, src, dst in ((2, "p2", "r2"), (4, "p5", "r5"), (6, "p7", "r7"), (7, "p8", "r8")):
        part_send_wait(ph, r[src], r[dst])
    for c in done:
        c.wait()


def body(latents, modulation, in_weight, out_weight, up_weight, down_weight, cotangent):
    vmem = pl.BlockSpec(memory_space=pltpu.VMEM)
    anywhere = pl.BlockSpec(memory_space=pl.ANY)
    out = lambda *s: jax.ShapeDtypeStruct(s, BF16)
    res, lgr, gu, gd, gi, gv = pl.pallas_call(
        kernel,
        out_shape=(out(2, 8, 8, D), out(2, 8, 8, D), out(5, 8, D), out(5, 8, D), out(5, 8, 768), out(5, 8, 768)),
        in_specs=[anywhere, anywhere, vmem, anywhere, anywhere, anywhere, anywhere],
        out_specs=(anywhere, anywhere, vmem, vmem, vmem, vmem),
        scratch_shapes=list(SPEC.values()),
        compiler_params=pltpu.CompilerParams(collective_id=0, has_side_effects=True, vmem_limit_bytes=67043328),
        name="block",
    )(
        latents.reshape(2, 8, 8, D),
        cotangent.reshape(2, 8, 8, D),
        modulation[0],
        jnp.transpose(in_weight, (1, 2, 0)),
        out_weight,
        up_weight,
        down_weight,
    )
    at = 4 * rem(lax.axis_index("seq"), 2)

    def own(g):
        rows = g.reshape(40, g.shape[-1])
        return jnp.where(at == 0, rows[:36], rows[4:])

    gi, gv = own(gi), own(gv)
    in_grad = jnp.concatenate([gi, gv[:, :WP]], axis=1).reshape(36, 3, WP)[:, :, :W]
    return (
        res.reshape(latents.shape),
        lgr.reshape(latents.shape),
        in_grad,
        gv[:, WP : WP + W].T,
        own(gu),
        own(gd).T,
    )


def solution(mesh):
    placed = (
        P("dp", "seq", "tensor", None),
        P("dp", None, None),
        P(None, None, "tensor"),
        P("tensor", None),
        P(None, "tensor"),
        P("tensor", None),
        P("dp", "seq", "tensor", None),
    )
    return jax.shard_map(
        body,
        mesh=mesh,
        in_specs=placed,
        out_specs=(
            P("dp", "seq", "tensor", None),
            P("dp", "seq", "tensor", None),
            P(("dp", "seq"), None, "tensor"),
            P("tensor", ("dp", "seq")),
            P(("dp", "seq"), "tensor"),
            P("tensor", ("dp", "seq")),
        ),
        check_vma=False,
    )
```

time: 407 us -> 167 us (0.41)
  Pallas kernels: 0 us -> 155 us
  waiting for transfers between devices: 129 us -> 0 us
  local copies, waits for them, and re-layouts: 78.8 us -> 6.06 us
  blocking collectives: 69.8 us -> 0 us
  matrix products: 55 us -> 0 us
  starting transfers between devices: 33.3 us -> 0 us
  other arithmetic: 21.2 us -> 2.71 us
  between operations: 16 us -> 0.67 us
    pallas_call x0 -> x1, Pallas kernels: none -> 155 us  [body(): pl.pallas_call(kernel, out_shape=(out(2, 8, 8, D), out(2, 8, 8, D), out(5...]
    unnamed x2 -> x0, waiting for transfers between devices: 72.7 us -> none
    all_to_all x4 -> x0, blocking collectives: 69.8 us -> none  [the longest x1 22.1 us: body(): lax.all_to_all(projected, 'seq', split_axis=2, concat_axis=1, tiled=True)]
    all_to_all x8 -> x0, waiting for transfers between devices: 56.8 us -> none  [the longest x3 34.1 us: sent_and_summed(): lax.all_to_all(pieces, axis, split_axis=0, concat_axis=0, tiled=True)]
    dot_general x17 -> x0, matrix products: 51.6 us -> none  [the longest x4 15.5 us: weight_grad(): lax.dot_general(left.reshape(-1, left.shape[-1]), right.reshape(-1, right...]
    all_to_all x8 -> x0, starting transfers between devices: 33 us -> none  [the longest x3 13.1 us: from_everyone(): lax.all_to_all(jnp.broadcast_to(array[None], (size, *array.shape)), axis,...]
    reshape x10 -> x1, local copies, waits for them, and re-layouts: 19.2 us -> 0.03 us  [body(): jnp.concatenate([gi, gv[:, :WP]], axis=1).reshape(36, 3, WP)[:, :, :W]]
    another operation x4 -> x0, local copies, waits for them, and re-layouts: 14.7 us -> none  [the longest x2 10.7 us: sum_packed(): lines = jnp.concatenate([b.reshape(size, -1) for b in pieces], axis=1)]
  transfers between devices with their start and end apart: 9 -> 0, of which waited for: 9 -> 0; matrix products, arithmetic and copies ran while one was open for 11% -> 0% of each run, Pallas kernels for 0% -> 0%
where the time goes in v1:
time: 167 us; the launch traced here: 164 us
  Pallas kernels  155 us (93%)
  local copies, waits for them, and re-layouts  6.06 us (4%)
  other arithmetic  2.71 us (2%)
    pallas_call x1, Pallas kernels, body(): pl.pallas_call(kernel, out_shape=(out(2, 8, 8, D), out(2, 8, 8, D), out(5...  155 us
    unnamed x4, local copies, waits for them, and re-layouts  5.41 us

profile of v1, /device:TPU:0, one launch (start us, length us, event | category | flops | bytes accessed | tf_op | source)
XLA Modules:
  0.0 164.3 jit_solution(706375124612131904)
XLA Ops:
  0.6 1.4 copy.17
  2.0 154.9 %block.1 = (bf16[2,8,8,1152]{3,2,1,0:T(8,128)(2,1)}, bf16[2,8,8,1152]{3,2,1,0:T(8,128)(2,1)}, bf16[5,8,1152]{2,1,0:T(8,128)(2,1)}, bf16[5,8,1152]{2,1,0:T(8,128)...) custom-call(bf16[2,8,8,1152]{3,2,1,0:T(8,128)(2,1)} %bitcast.23, bf16[2,8,8,1152]{3,2,1,0:T(8,128)(2,1)} %bitcast.24, ...), custom_call_target="tpu_custom_call" | custom-call | tf_op jit(solution)/shard_map/block/pallas_call | solution.py:525
  156.9 1.0 slice_select_fusion.2
  157.9 0.7 copy.14
  158.6 0.6 slice_bitcast_fusion
  159.2 1.7 %fusion = (bf16[1152,36]{0,1:T(8,128)(2,1)}, bf16[36,1152]{1,0:T(8,128)(2,1)}) fusion(bf16[40,1152]{1,0:T(8,128)(2,1)} %bitcast.20, pred[]{:T(512)S(6)} %eq.2, bf16[40,1152]{1,0:T(8,128)(2,1)} %bitcast.19), kind=kLoop, calls=%fused_computation.1 | loop fusion | flops 82944 | bytes 497665 | tf_op jit(solution)/shard_map/transpose | solution.py:556
  161.0 1.7 %copy.20 = bf16[1,2,64,1152]{3,2,1,0:T(8,128)(2,1)} copy(bf16[1,2,64,1152]{3,2,1,0:T(8,128)(2,1)} %bitcast.22) | data formatting | bytes 589824
  162.6 1.7 %copy.21 = bf16[1,2,64,1152]{3,2,1,0:T(8,128)(2,1)} copy(bf16[1,2,64,1152]{3,2,1,0:T(8,128)(2,1)} %bitcast.21) | data formatting | bytes 589824
  (3 shorter events, 0.0 us)

commit v2 on v1

--- a/solution.py
+++ b/solution.py
@@ -57,18 +57,18 @@
     vm = lambda *s, t=BF16: pltpu.VMEM(s, t)
     dma = lambda *s: pltpu.SemaphoreType.DMA(s)
     spec = {
-        "xs": vm(8, 2, 8, D), "cs": vm(8, 2, 8, D),
+        "xs": vm(8, 2, 8, D), "cy": vm(4, 2, 8, 8, D), "cg": vm(4, 8, 2, 8, D),
         "win": vm(3, WP, D), "wout": vm(WP, D), "wup": vm(D, D), "wdown": vm(D, D),
         "f": vm(4, 128, D), "s": vm(4, 128, D), "g": vm(4, 128, D), "a": vm(4, 128, D),
-        "p2": vm(4, 128, D), "p5": vm(4, 128, D), "p7": vm(4, 128, D), "p8": vm(4, 128, D),
-        "r2": vm(4, 128, D), "r5": vm(4, 128, D), "r7": vm(4, 128, D), "r8": vm(4, 128, D),
+        "p2": vm(4, 128, D), "p5": vm(4, 128, D), "p8": vm(4, 128, D), "ag": vm(4, 128, D, t=F32),
+        "r2": vm(4, 128, D), "r5": vm(4, 128, D), "r8": vm(4, 128, D),
         "qkv": vm(4, 128, 3 * WP), "probs": vm(4, 512, 128, t=F32), "att": vm(4, 128, WP),
         "act": vm(4, 128, D), "hg": vm(4, 128, D), "dqkv": vm(4, 128, 3 * WP),
         "mid": vm(128, D, t=F32), "mg": vm(128, D, t=F32),
         "ro": vm(8, 2, 8, D), "lo": vm(8, 2, 8, D), "rl": vm(2, 8, 8, D), "ll": vm(2, 8, 8, D),
         "wsem": dma(6),
-        "ys": dma(8, 4), "yr": dma(8, 4),
-        "ss": dma(4, 8), "sr": dma(4, 8),
+        "ys": dma(8, 6), "yr": dma(8, 6),
+        "ss": dma(7, 8), "sr": dma(7, 8),
         "osem": dma(2),
         "js": dma(4, 7), "jr": dma(4, 7),
     }
@@ -88,7 +88,7 @@
 SPEC = scratch_spec()
 
 
-def kernel(lat, cot, mod, in_w, out_w, up_w, down_w, res, lgr, gu, gd, gi, gv, *scratch):
+def kernel(lat, cot, mod, in_w, out_w, up_w, down_w, res, lgr, gu, gd, gi, go, *scratch):
     r = dict(zip(SPEC, scratch))
     dp, seq, me = lax.axis_index("dp"), lax.axis_index("seq"), lax.axis_index("tensor")
     core, z_lo = rem(dp, 2), div(dp, 2)
@@ -131,16 +131,54 @@
         pl.semaphore_signal(barrier, inc=1, device_id=where, device_id_type=MESH)
     pl.semaphore_wait(barrier, len(peers))
 
-    sends = []
+    PARTS_C = (lambda v: v.at[0], lambda v: v.at[1])
+    PARTS_T = (lambda v: v.at[pl.ds(0, 64)], lambda v: v.at[pl.ds(64, 64)])
+
+    def hop(ph, buf, parts, src, k, half, n, to):
+        t = rem(me + k, 4)
+        piece = parts[half](buf.at[t])
+        return remote(piece if src is None else parts[half](src), piece, r["ys"].at[ph, n], r["yr"].at[ph, n], y_peer(to))
+
+    HOPS = ((0, 0, 0, 1), (0, 1, 2, 3), (0, 1, 1, 1), (0, 0, 3, 3))
+    PASS = ((3, 0, 4, 1), (1, 1, 5, 3))
+
+    def gather_start(ph, src, buf, parts):
+        for k, half, n, to in HOPS:
+            hop(ph, buf, parts, src, k, half, n, to).start()
+
+    def gather_pass(ph, buf, parts):
+        for n, half, frm, (k, _, m, to) in ((0, 0, 3, PASS[0]), (2, 1, 1, PASS[1])):
+            hop(ph, buf, parts, None, frm, half, n, 1).wait_recv()
+            hop(ph, buf, parts, None, k, half, m, to).start()
+
+    def gather_left(ph, buf, parts):
+        hop(ph, buf, parts, None, 3, 1, 1, 1).wait_recv()
+
+    def gather_right(ph, buf, parts):
+        hop(ph, buf, parts, None, 1, 0, 3, 1).wait_recv()
+
+    def gather_far(ph, buf, parts):
+        hop(ph, buf, parts, None, 2, 0, 4, 1).wait_recv()
+        hop(ph, buf, parts, None, 2, 1, 5, 1).wait_recv()
+
+    def gather_sent(ph, src, buf, parts):
+        for k, half, n, to in HOPS:
+            hop(ph, buf, parts, src, k, half, n, to).wait_send()
+        for k, half, n, to in PASS:
+            hop(ph, buf, parts, None, k, half, n, to).wait_send()
 
     def exchange_in(row, src, dst):
         for k in range(1, 8):
             to = rem(seq + k, 8)
             c = remote(src.at[:, to], dst.at[seq], r["ss"].at[row, k], r["sr"].at[row, k], seq_peer(k))
             c.start()
-            sends.append(c)
         c = local(src.at[:, seq], dst.at[seq], r["sr"].at[row, 0])
         c.start()
+
+    def exchange_in_sent(row, src, dst):
+        for k in range(1, 8):
+            to = rem(seq + k, 8)
+            remote(src.at[:, to], dst.at[seq], r["ss"].at[row, k], r["sr"].at[row, k], seq_peer(k)).wait_send()
 
     def exchange_in_wait(row, src, dst):
         local(src.at[:, seq], dst.at[seq], r["sr"].at[row, 0]).wait()
@@ -149,7 +187,8 @@
             remote(src.at[:, frm], dst.at[frm], r["ss"].at[row, k], r["sr"].at[row, k], seq_peer(k)).wait_recv()
 
     exchange_in(0, lat, r["xs"])
-    exchange_in(1, cot, r["cs"])
+    gather_start(1, cot, r["cy"], PARTS_C)
+    exchange_in(3, cot, r["cg"].at[me])
     for c in weights:
         c.start()
     for j in range(3):
@@ -157,20 +196,10 @@
     r["wout"][W:] = jnp.zeros((WP - W, D), BF16)
 
     def row(i):
-        return mod[i : i + 1, :]
+        return mod[i]
 
     def halves(ref, h):
         return ref[4 * h : 4 * h + 4].astype(F32).reshape(64, D)
-
-    def gather_start(ph, buf):
-        for k in (2, 1, 3):
-            c = remote(buf.at[me], buf.at[me], r["ys"].at[ph, k], r["yr"].at[ph, k], y_peer(k))
-            c.start()
-            sends.append(c)
-
-    def gather_wait(ph, buf, k):
-        frm = rem(me + 4 - k, 4)
-        remote(buf.at[frm], buf.at[frm], r["ys"].at[ph, k], r["yr"].at[ph, k], y_peer(k)).wait_recv()
 
     def part_send(ph, src, dst, k):
         to = rem(me + k, 4)
@@ -193,21 +222,31 @@
             total = total + dst[rem(me + k, 4), rows, :].astype(F32)
         return total
 
+    ORDER = (0, 3, 1, 2)
+
     def block_of(i):
-        k = jnp.where(i < 2, i, 5 - i)
+        k = jnp.where(i == 1, 3, jnp.maximum(i - 1, 0))
         return k, rem(me + k, 4)
 
     def arrival(ph, buf, i):
-        for j, k in ((1, 1), (2, 3), (3, 2)):
+        @pl.when(i == 1)
+        def _():
+            gather_pass(ph, buf, PARTS_T)
+            gather_left(ph, buf, PARTS_T)
+
+        @pl.when(i == 2)
+        def _():
+            gather_right(ph, buf, PARTS_T)
+
+        @pl.when(i == 3)
+        def _():
+            gather_far(ph, buf, PARTS_T)
+
+    def part_out(ph, src, dst, i):
+        for j in (1, 2, 3):
             @pl.when(i == j)
             def _():
-                gather_wait(ph, buf, 4 - k)
-
-    def part_out(ph, src, dst, i):
-        for j, k in ((1, 1), (2, 3), (3, 2)):
-            @pl.when(i == j)
-            def _():
-                part_send(ph, src, dst, k)
+                part_send(ph, src, dst, ORDER[j])
 
     lane = lax.broadcasted_iota(jnp.int32, (128, WP), 1)
     head_masks = [(lane >= HEAD_DIM * h) & (lane < HEAD_DIM * (h + 1)) for h in range(HEADS)]
@@ -220,16 +259,12 @@
     def side_by_side(v):
         return jnp.concatenate([v[128 * h : 128 * h + 128] for h in range(HEADS)], axis=1)
 
+    gather_pass(1, r["cy"], PARTS_C)
     exchange_in_wait(0, lat, r["xs"])
     for h in range(2):
         normed, _ = norm(halves(r["xs"], h))
         r["f"][me, 64 * h : 64 * h + 64, :] = (normed * (1.0 + row(1)) + row(0)).astype(BF16)
-    gather_start(0, r["f"])
-    exchange_in_wait(1, cot, r["cs"])
-    for h in range(2):
-        r["g"][me, 64 * h : 64 * h + 64, :] = (row(5) * halves(r["cs"], h)).astype(BF16)
-
-    gather_start(1, r["g"])
+    gather_start(0, None, r["f"], PARTS_T)
     for c in weights[:4]:
         c.wait()
 
@@ -254,8 +289,38 @@
         part_out(2, r["p2"], r["r2"], i)
         return carry
 
-    lax.fori_loop(0, 4, attend_block, 0)
+    lax.fori_loop(0, 1, attend_block, 0)
+
+    gather_left(1, r["cy"], PARTS_C)
+    exchange_in(1 + 1, r["cy"].at[rem(me + 3, 4)], r["cg"].at[rem(me + 3, 4)])
+    gather_right(1, r["cy"], PARTS_C)
+    exchange_in(1 + 3, r["cy"].at[rem(me + 1, 4)], r["cg"].at[rem(me + 1, 4)])
+    lax.fori_loop(1, 3, attend_block, 0)
+    gather_far(1, r["cy"], PARTS_C)
+    exchange_in(1 + 0, r["cy"].at[rem(me + 2, 4)], r["cg"].at[rem(me + 2, 4)])
+    lax.fori_loop(3, 4, attend_block, 0)
+
+    def branch_block(k, row_, src):
+        t = rem(me + k, 4)
+        exchange_in_wait(row_, src, r["cg"].at[t])
+        for h in range(2):
+            r["g"][t, 64 * h : 64 * h + 64, :] = (row(5) * r["cg"][t, 4 * h : 4 * h + 4].astype(F32).reshape(64, D)).astype(BF16)
+
+    branch_block(0, 3, cot)
+    branch_block(3, 2, r["cy"].at[rem(me + 3, 4)])
+    branch_block(1, 4, r["cy"].at[rem(me + 1, 4)])
+    branch_block(2, 1, r["cy"].at[rem(me + 2, 4)])
+    weights[4].wait()
+    weights[5].wait()
+
+    def branch_back(n, c):
+        cols = pl.ds(pl.multiple_of(n * 384, 384), 384)
+        r["ag"][:, :, cols] = dot(r["g"][...].reshape(512, D), r["wdown"][cols, :], NT).reshape(4, 128, 384)
+        return c
+
+    lax.fori_loop(0, 3, branch_back, 0)
     part_wait(2, r["p2"], r["r2"])
+    part_send_wait(2, r["p2"], r["r2"])
 
     for h in range(2):
         rows = slice(64 * h, 64 * h + 64)
@@ -263,20 +328,16 @@
         r["mid"][rows, :] = midway
         normed, _ = norm(midway)
         r["s"][me, rows, :] = (normed * (1.0 + row(4)) + row(3)).astype(BF16)
-    gather_start(3, r["s"])
-
-    weights[4].wait()
-    weights[5].wait()
+    gather_start(3, None, r["s"], PARTS_T)
 
     def mlp_block(i, carry):
         k, t = block_of(i)
         arrival(3, r["s"], i)
-        arrival(1, r["g"], i)
 
         def hidden_cols(n, c):
             cols = pl.ds(pl.multiple_of(n * 384, 384), 384)
             v = dot(r["s"][t], r["wup"][:, cols], NN)
-            ag = dot(r["g"][t], r["wdown"][cols, :], NT)
+            ag = r["ag"][t, :, cols]
             th = jnp.tanh(GELU_C * (v + 0.044715 * (v * v * v)))
             r["act"][t, :, cols] = (0.5 * v * (1.0 + th)).astype(BF16)
             slope = 0.5 * (1.0 + th) + (0.5 * v) * ((1.0 - th * th) * (GELU_C * (1.0 + (3.0 * 0.044715) * (v * v))))
@@ -292,13 +353,6 @@
 
         lax.fori_loop(0, 3, grad_cols, 0)
         part_out(4, r["p5"], r["r5"], i)
-
-        def result_cols(n, c):
-            cols = pl.ds(pl.multiple_of(n * 384, 384), 384)
-            r["p8"][t, :, cols] = dot(r["act"][t], r["wdown"][:, cols], NN).astype(BF16)
-            return c
-
-        lax.fori_loop(0, 3, result_cols, 0)
         return carry
 
     lax.fori_loop(0, 4, mlp_block, 0)
@@ -386,7 +440,7 @@
             else:
                 remote(src, r["C" + name].at[frm], r["js"].at[index, 3 + k], r["jr"].at[index, 3 + k], where).wait()
 
-    def job_second_sum(index, out):
+    def job_second_sum(index):
         name, n, x_first = JOBS[index]
         if x_first:
             total = r["H" + name][z_lo, pl.ds(4 * z_hi, 5)].astype(F32)
@@ -396,32 +450,46 @@
             at = x
         for k in (1, 2, 3):
             total = total + r["C" + name][rem(at + k, 4)].astype(F32)
-        out[...] = total.astype(BF16)
+        total = total.reshape(40, n)
+        return jnp.where(z_hi == 0, total[:36], total[4:]).astype(BF16)
 
     weight_grad(r["s"], lambda: r["hg"][...], D, "u", 0)
     job_core(0, True)
+    weight_grad(r["g"], lambda: r["act"][...], D, "d", 0)
+    job_core(1, True)
+    job_core(0, False)
+    job_core_sum(0)
+    job_first(0, True)
+
+    def result_block(i, carry):
+        t = rem(me + i, 4)
+
+        def result_cols(n, c):
+            cols = pl.ds(pl.multiple_of(n * 384, 384), 384)
+            r["p8"][t, :, cols] = dot(r["act"][t], r["wdown"][:, cols], NN).astype(BF16)
+            return c
+
+        lax.fori_loop(0, 3, result_cols, 0)
+        return carry
 
     part_wait(4, r["p5"], r["r5"])
     for h in range(2):
         rows = slice(64 * h, 64 * h + 64)
         normed, inverse = norm(r["mid"][rows, :])
         back = norm_back(normed, inverse, part_sum(r["p5"], r["r5"], h) * (1.0 + row(4)))
-        mg = halves(r["cs"], h) + back
+        mg = r["cg"][me, 4 * h : 4 * h + 4].astype(F32).reshape(64, D) + back
         r["mg"][rows, :] = mg
         r["a"][me, rows, :] = (row(2) * mg).astype(BF16)
-    gather_start(5, r["a"])
-    for k in (1, 3, 2):
-        part_send(7, r["p8"], r["r8"], k)
-
-    weight_grad(r["g"], lambda: r["act"][...], D, "d", 0)
-    job_core(1, True)
-    job_core(0, False)
-    job_core_sum(0)
-    job_first(0, True)
+    gather_start(5, None, r["a"], PARTS_T)
+    job_core(1, False)
+    job_core_sum(1)
+    job_first(1, True)
+    lax.fori_loop(0, 2, result_block, 0)
 
     def attend_back_block(i, carry):
         k, t = block_of(i)
         arrival(5, r["a"], i)
+
         grad = dot(r["a"][t], r["wout"][...], NT).astype(BF16)
         q, kk, v = (r["qkv"][t, :, j * WP : (j + 1) * WP] for j in range(3))
         qs, gs = stacked(q), stacked(grad)
@@ -438,21 +506,29 @@
             total = dot(r["dqkv"][t, :, 0:WP], r["win"][0, :, cols], NN)
             for j in (1, 2):
                 total = total + dot(r["dqkv"][t, :, j * WP : (j + 1) * WP], r["win"][j, :, cols], NN)
-            r["p7"][t, :, cols] = total.astype(BF16)
-        part_out(6, r["p7"], r["r7"], i)
+            r["p2"][t, :, cols] = total.astype(BF16)
+        part_out(6, r["p2"], r["r2"], i)
         return carry
 
-    lax.fori_loop(0, 2, attend_back_block, 0)
-    job_core(1, False)
-    job_core_sum(1)
-    job_first(1, True)
-    lax.fori_loop(2, 4, attend_back_block, 0)
+    lax.fori_loop(0, 1, attend_back_block, 0)
+    lax.fori_loop(1, 4, attend_back_block, 0)
 
     weight_grad(r["f"], lambda: r["dqkv"][:, :, 0:768], 768, "i", 0)
     job_core(2, True)
     weight_grad(r["f"], lambda: r["dqkv"][:, :, 768:1152], 384, "v", 0)
     weight_grad(r["a"], lambda: r["att"][...], 384, "v", 384)
     job_core(3, True)
+    for index in (0, 1):
+        job_first(index, False)
+        job_first_sum(index)
+        job_second(index, True)
+    lax.fori_loop(2, 4, result_block, 0)
+    for k in (1, 3, 2):
+        part_send(7, r["p8"], r["r8"], k)
+    for index in (2, 3):
+        job_core(index, False)
+        job_core_sum(index)
+        job_first(index, True)
 
     def exchange_out(row_, src, dst):
         for k in range(1, 8):
@@ -466,53 +542,57 @@
             frm = rem(seq + 8 - k, 8)
             remote(src.at[frm], dst.at[:, frm], r["ss"].at[row_, k], r["sr"].at[row_, k], seq_peer(k)).wait()
 
+    part_wait(6, r["p2"], r["r2"])
+    for h in range(2):
+        rows = slice(64 * h, 64 * h + 64)
+        normed, inverse = norm(halves(r["xs"], h))
+        back = norm_back(normed, inverse, part_sum(r["p2"], r["r2"], h) * (1.0 + row(1)))
+        out = r["mg"][rows, :] + back
+        r["lo"][4 * h : 4 * h + 4] = out.astype(BF16).reshape(4, 2, 8, D)
+    exchange_out(6, r["lo"], r["ll"])
+
+    for index, out in ((0, gu), (1, gd)):
+        job_second(index, False)
+        out[...] = job_second_sum(index)
+    job_first(2, False)
+    job_first_sum(2)
+    job_second(2, True)
+
     part_wait(7, r["p8"], r["r8"])
     for h in range(2):
         rows = slice(64 * h, 64 * h + 64)
         out = r["mid"][rows, :] + row(5) * part_sum(r["p8"], r["r8"], h)
         r["ro"][4 * h : 4 * h + 4] = out.astype(BF16).reshape(4, 2, 8, D)
-    exchange_out(2, r["ro"], r["rl"])
-
-    job_first(0, False)
-    job_first_sum(0)
-    job_second(0, True)
-
-    part_wait(6, r["p7"], r["r7"])
-    for h in range(2):
-        rows = slice(64 * h, 64 * h + 64)
-        normed, inverse = norm(halves(r["xs"], h))
-        back = norm_back(normed, inverse, part_sum(r["p7"], r["r7"], h) * (1.0 + row(1)))
-        out = r["mg"][rows, :] + back
-        r["lo"][4 * h : 4 * h + 4] = out.astype(BF16).reshape(4, 2, 8, D)
-    exchange_out(3, r["lo"], r["ll"])
-
-    job_first(1, False)
-    job_first_sum(1)
-    job_second(1, True)
-    for index in (2, 3):
-        job_core(index, False)
-        job_core_sum(index)
-        job_first(index, True)
-    job_second(0, False)
-    job_second_sum(0, gu)
-    job_second(1, False)
-    job_second_sum(1, gd)
-    exchange_out_wait(2, r["ro"], r["rl"])
-    done = [local(r["rl"], res, r["osem"].at[0])]
-    done[0].start()
-    for index in (2, 3):
-        job_first(index, False)
-        job_first_sum(index)
-        job_second(index, True)
-    exchange_out_wait(3, r["lo"], r["ll"])
-    done.append(local(r["ll"], lgr, r["osem"].at[1]))
-    done[1].start()
-    for index, out in ((2, gi), (3, gv)):
-        job_second(index, False)
-        job_second_sum(index, out)
-    for c in sends:
-        c.wait_send()
-    for ph, src, dst in ((2, "p2", "r2"), (4, "p5", "r5"), (6, "p7", "r7"), (7, "p8", "r8")):
+    exchange_out(5, r["ro"], r["rl"])
+
+    job_first(3, False)
+    job_first_sum(3)
+    job_second(3, True)
+    exchange_out_wait(6, r["lo"], r["ll"])
+    exchange_out_wait(5, r["ro"], r["rl"])
+    done = [local(r["rl"], res, r["osem"].at[0]), local(r["ll"], lgr, r["osem"].at[1])]
+    for c in done:
+        c.start()
+    job_second(2, False)
+    part = job_second_sum(2)
+    gi[0] = part[:, :W]
+    gi[1] = part[:, WP : WP + W]
+    job_second(3, False)
+    part = job_second_sum(3)
+    gi[2] = part[:, :W]
+    go[...] = part[:, WP : WP + W]
+    for row_, src, dst in (
+        (0, lat, r["xs"]),
+        (3, cot, r["cg"].at[me]),
+        (2, r["cy"].at[rem(me + 3, 4)], r["cg"].at[rem(me + 3, 4)]),
+        (4, r["cy"].at[rem(me + 1, 4)], r["cg"].at[rem(me + 1, 4)]),
+        (1, r["cy"].at[rem(me + 2, 4)], r["cg"].at[rem(me + 2, 4)]),
+    ):
+        exchange_in_sent(row_, src, dst)
+    gather_sent(1, cot, r["cy"], PARTS_C)
+    for ph, buf in ((0, "f"), (3, "s"), (5, "a")):
+        gather_sent(ph, None, r[buf], PARTS_T)
+    for ph, src, dst in ((4, "p5", "r5"), (6, "p2", "r2"), (7, "p8", "r8")):
         part_send_wait(ph, r[src], r[dst])
     for c in done:
         c.wait()
@@ -522,9 +602,10 @@
     vmem = pl.BlockSpec(memory_space=pltpu.VMEM)
     anywhere = pl.BlockSpec(memory_space=pl.ANY)
     out = lambda *s: jax.ShapeDtypeStruct(s, BF16)
-    res, lgr, gu, gd, gi, gv = pl.pallas_call(
+    shapes = (out(2, 8, 8, D), out(2, 8, 8, D), out(36, D), out(36, D), out(3, 36, W), out(36, W))
+    found = pl.pallas_call(
         kernel,
-        out_shape=(out(2, 8, 8, D), out(2, 8, 8, D), out(5, 8, D), out(5, 8, D), out(5, 8, 768), out(5, 8, 768)),
+        out_shape=shapes,
         in_specs=[anywhere, anywhere, vmem, anywhere, anywhere, anywhere, anywhere],
         out_specs=(anywhere, anywhere, vmem, vmem, vmem, vmem),
         scratch_shapes=list(SPEC.values()),
@@ -533,28 +614,41 @@
     )(
         latents.reshape(2, 8, 8, D),
         cotangent.reshape(2, 8, 8, D),
-        modulation[0],
+        jnp.transpose(modulation, (1, 0, 2)),
         jnp.transpose(in_weight, (1, 2, 0)),
         out_weight,
         up_weight,
         down_weight,
     )
-    at = 4 * rem(lax.axis_index("seq"), 2)
-
-    def own(g):
-        rows = g.reshape(40, g.shape[-1])
-        return jnp.where(at == 0, rows[:36], rows[4:])
-
-    gi, gv = own(gi), own(gv)
-    in_grad = jnp.concatenate([gi, gv[:, :WP]], axis=1).reshape(36, 3, WP)[:, :, :W]
+    res, lgr, gu, gd, gi, go = pl.pallas_call(
+        hand_over,
+        out_shape=shapes,
+        in_specs=[anywhere] * 6,
+        out_specs=(anywhere,) * 6,
+        scratch_shapes=[pltpu.VMEM(v.shape, BF16) for v in shapes] + [pltpu.SemaphoreType.DMA((2, 6))],
+        name="hand_over",
+    )(*found)
     return (
         res.reshape(latents.shape),
         lgr.reshape(latents.shape),
-        in_grad,
-        gv[:, WP : WP + W].T,
-        own(gu),
-        own(gd).T,
+        jnp.transpose(gi, (1, 0, 2)),
+        go.T,
+        gu,
+        gd.T,
     )
+
+
+def hand_over(*refs):
+    given, outs, held, sems = refs[:6], refs[6:12], refs[12:18], refs[18]
+    into = [pltpu.make_async_copy(a, b, sems.at[0, i]) for i, (a, b) in enumerate(zip(given, held))]
+    back = [pltpu.make_async_copy(a, b, sems.at[1, i]) for i, (a, b) in enumerate(zip(held, outs))]
+    for c in into:
+        c.start()
+    for c, d in zip(into, back):
+        c.wait()
+        d.start()
+    for d in back:
+        d.wait()
 
 
 def solution(mesh):

time: 167 us -> 119 us (0.71); the launches traced: 164 us -> 119 us
  Pallas kernels: 155 us -> 118 us
  local copies, waits for them, and re-layouts: 6.06 us -> 0 us
  other arithmetic: 2.71 us -> 0 us
    pallas_call x1 -> x2, Pallas kernels: 155 us -> 118 us  [the longest x1 116 us: body(): pl.pallas_call(kernel, out_shape=shapes, in_specs=[anywhere, anywhere, vm...]
    unnamed x4 -> x0, local copies, waits for them, and re-layouts: 5.41 us -> none
    transpose x1 -> x0, other arithmetic: 1.74 us -> none  [body(): own(gd)]
where the time goes in v2:
time: 119 us
  Pallas kernels  118 us (99%)
    pallas_call x1, Pallas kernels, body(): pl.pallas_call(kernel, out_shape=shapes, in_specs=[anywhere, anywhere, vm...  116 us

profile of v2, /device:TPU:0, one launch (start us, length us, event | category | flops | bytes accessed | tf_op | source)
XLA Modules:
  0.0 118.6 jit_solution(11010535695293469904)
XLA Ops:
  0.6 116.0 %block.1 = (bf16[2,8,8,1152]{3,2,1,0:T(8,128)(2,1)}, bf16[2,8,8,1152]{3,2,1,0:T(8,128)(2,1)}, bf16[36,1152]{1,0:T(8,128)(2,1)}, bf16[36,1152]{1,0:T(8,128)(2,1)}...) custom-call(bf16[2,8,8,1152]{3,2,1,0:T(8,128)(2,1)} %bitcast.10, bf16[2,8,8,1152]{3,2,1,0:T(8,128)(2,1)} %bitcast.11, ...), custom_call_target="tpu_custom_call" | custom-call | tf_op jit(solution)/shard_map/block/pallas_call | solution.py:606
  116.6 2.0 %hand_over.1 = (bf16[2,8,8,1152]{3,2,1,0:T(8,128)(2,1)}, bf16[2,8,8,1152]{3,2,1,0:T(8,128)(2,1)}, bf16[36,1152]{1,0:T(8,128)(2,1)}, bf16[36,1152]{1,0:T(8,128)(2...) custom-call(bf16[2,8,8,1152]{3,2,1,0:T(8,128)(2,1)} %get-tuple-element.18.refs_0_, ...), custom_call_target="tpu_custom_call" | custom-call | tf_op jit(solution)/shard_map/hand_over/pallas_call | solution.py:623

commit v3 on v2

v3 whole, which is shorter than its diff:
```python
import math

import jax
import jax.numpy as jnp
from jax import lax
from jax.experimental import pallas as pl
from jax.experimental.pallas import tpu as pltpu
from jax.sharding import PartitionSpec as P

HEAD_DIM = 72
HEADS = 4
D = 1152
W = 288
WP = 384
SCALE = 1.0 / math.sqrt(HEAD_DIM)
EPS = 1e-6
MESH = pl.DeviceIdType.MESH
F32 = jnp.float32
BF16 = jnp.bfloat16
GELU_C = math.sqrt(2.0 / math.pi)

NN = (((1,), (0,)), ((), ()))
NT = (((1,), (1,)), ((), ()))
TN = (((0,), (0,)), ((), ()))


def rem(a, b):
    return lax.rem(a, b)


def div(a, b):
    return lax.div(a, b)


def dot(a, b, dims):
    return lax.dot_general(a, b, dims, preferred_element_type=F32)


def norm(rows):
    center = jnp.mean(rows, axis=-1, keepdims=True)
    centred = rows - center
    spread = jnp.mean(centred * centred, axis=-1, keepdims=True)
    inverse = lax.rsqrt(spread + EPS)
    return centred * inverse, inverse


def norm_back(normed, inverse, up):
    mean_grad = jnp.mean(up, axis=-1, keepdims=True)
    mean_cross = jnp.mean(up * normed, axis=-1, keepdims=True)
    return (up - mean_grad - normed * mean_cross) * inverse


JOBS = (("u", 1152, True), ("d", 1152, False), ("o", 640, True), ("p", 512, False), ("i", 512, True), ("v", 384, False))
CI = 896


def scratch_spec():
    vm = lambda *s, t=BF16: pltpu.VMEM(s, t)
    dma = lambda *s: pltpu.SemaphoreType.DMA(s)
    spec = {
        "xs": vm(8, 2, 8, D), "cy": vm(4, 2, 8, 8, D), "cg": vm(4, 8, 2, 8, D),
        "win": vm(3, WP, D), "wo": vm(4, 48, 8, D), "wup": vm(D, D), "wdown": vm(D, D),
        "f": vm(4, 128, D), "s": vm(4, 128, D), "g": vm(4, 128, D), "ao": vm(128, D),
        "p5": vm(4, 128, D), "p7": vm(4, 128, D), "ag": vm(4, 128, D, t=F32),
        "r5": vm(4, 128, D), "r7": vm(4, 128, D), "r8": vm(4, 128, D),
        "qkv": vm(4, 128, 3 * WP), "probs": vm(4, 512, 128, t=F32),
        "as": vm(4, 128, WP), "at": vm(4, 128, WP), "ds": vm(4, 128, WP), "da": vm(4, 128, WP), "attc": vm(128, D),
        "act": vm(4, 128, D), "hg": vm(4, 128, D), "dqkv": vm(4, 128, 3 * WP), "dqc": vm(4, 128, CI),
        "mid": vm(128, D, t=F32), "mg": vm(128, D, t=F32),
        "ro": vm(8, 2, 8, D), "lo": vm(8, 2, 8, D), "rl": vm(2, 8, 8, D), "ll": vm(2, 8, 8, D),
        "oy": vm(4, 40, WP), "or": vm(4, 40, WP),
        "wsem": dma(6),
        "ys": dma(10, 6), "yr": dma(10, 6),
        "ss": dma(7, 8), "sr": dma(7, 8),
        "osem": dma(2),
        "js": dma(6, 7), "jr": dma(6, 7),
        "ws": dma(4, 4), "wr": dma(4, 4),
    }
    for name, n, x_first in JOBS:
        spec["G" + name] = vm(2, 2, 4, 9, 8, n)
        spec["A" + name] = vm(2, 4, 9, 8, n)
        if x_first:
            spec["B" + name] = vm(3, 2, 9, 8, n)
            spec["H" + name] = vm(2, 9, 8, n)
        else:
            spec["B" + name] = vm(3, 4, 5, 8, n)
            spec["H" + name] = vm(4, 5, 8, n)
        spec["C" + name] = vm(3, 5, 8, n)
    return spec


SPEC = scratch_spec()

TO = {1: 3, 2: 1, 3: 2}
BACK = {1: 2, 2: 1, 3: 3}
HOPS = ((0, 1, 0, 1), (1, 1, 0, 1), (1, 3, 0, 2), (0, 3, 0, 2), (0, 1, 1, 3), (1, 3, 2, 3))
PARTS_C = (lambda v: v.at[0], lambda v: v.at[1])
PARTS_T = (lambda v: v.at[pl.ds(0, 64)], lambda v: v.at[pl.ds(64, 64)])


def kernel(lat, cot, mod, in_w, out_w, up_w, down_w, res, lgr, gu, gd, gi, go, *scratch):
    r = dict(zip(SPEC, scratch))
    dp, seq, me = lax.axis_index("dp"), lax.axis_index("seq"), lax.axis_index("tensor")
    core, z_lo = rem(dp, 2), div(dp, 2)
    x, z_hi = div(seq, 2), rem(seq, 2)
    z = z_hi * 2 + z_lo

    def remote(src, dst, send, recv, where):
        return pltpu.make_async_remote_copy(src_ref=src, dst_ref=dst, send_sem=send, recv_sem=recv, device_id=where, device_id_type=MESH)

    def local(src, dst, sem):
        return pltpu.make_async_copy(src, dst, sem)

    def seq_peer(k):
        return (dp, rem(seq + k, 8), me)

    def y_peer(k):
        return (dp, seq, rem(me + k, 4))

    def core_peer():
        return (dp + 1 - 2 * core, seq, me)

    def x_peer(k):
        return (dp, rem(x + k, 4) * 2 + z_hi, me)

    def z_peer(k):
        other = rem(z + k, 4)
        return (rem(other, 2) * 2 + core, x * 2 + div(other, 2), me)

    weights = [local(in_w.at[j], r["win"].at[j, pl.ds(0, W)], r["wsem"].at[j]) for j in range(3)]
    weights += [
        local(out_w, r["wo"].at[0, pl.ds(0, 36)], r["wsem"].at[3]),
        local(up_w, r["wup"], r["wsem"].at[4]),
        local(down_w, r["wdown"], r["wsem"].at[5]),
    ]

    barrier = pltpu.get_barrier_semaphore()
    peers = [seq_peer(k) for k in range(1, 8)] + [y_peer(k) for k in range(1, 4)] + [core_peer()]
    peers += [z_peer(1), z_peer(3)]
    for where in peers:
        pl.semaphore_signal(barrier, inc=1, device_id=where, device_id_type=MESH)
    pl.semaphore_wait(barrier, len(peers))

    def hop(ph, buf, parts, n, src=None):
        half, to, at, there = HOPS[n]
        given = buf.at[at] if src is None or at else src
        return remote(parts[half](given), parts[half](buf.at[there]), r["ys"].at[ph, n], r["yr"].at[ph, n], y_peer(to))

    def gather_start(ph, buf, parts, src=None, hops=(0, 2, 1, 3)):
        for n in hops:
            hop(ph, buf, parts, n, src).start()

    def gather_pass(ph, buf, parts):
        hop(ph, buf, parts, 0).wait_recv()
        hop(ph, buf, parts, 4).start()
        hop(ph, buf, parts, 2).wait_recv()
        hop(ph, buf, parts, 5).start()

    def gather_near(ph, buf, parts):
        hop(ph, buf, parts, 1).wait_recv()
        hop(ph, buf, parts, 3).wait_recv()

    def gather_far(ph, buf, parts):
        hop(ph, buf, parts, 4).wait_recv()
        hop(ph, buf, parts, 5).wait_recv()

    def gather_sent(ph, buf, parts, src=None):
        for n in range(6):
            hop(ph, buf, parts, n, src).wait_send()

    def part(ph, src, dst, k):
        return remote(src.at[k], dst.at[BACK[k]], r["ys"].at[ph, k], r["yr"].at[ph, BACK[k]], y_peer(TO[k]))

    def part_wait(ph, src, dst, slots=(1, 2, 3)):
        for k in slots:
            part(ph, src, dst, BACK[k]).wait_recv()

    def part_send_wait(ph, src, dst):
        for k in (1, 2, 3):
            part(ph, src, dst, k).wait_send()

    def part_sum(src, dst, h):
        rows = slice(64 * h, 64 * h + 64)
        total = src[0, rows, :].astype(F32)
        for k in (1, 2, 3):
            total = total + dst[k, rows, :].astype(F32)
        return total

    def exchange_in(row_, src, dst):
        for k in range(1, 8):
            to = rem(seq + k, 8)
            remote(src.at[:, to], dst.at[seq], r["ss"].at[row_, k], r["sr"].at[row_, k], seq_peer(k)).start()
        local(src.at[:, seq], dst.at[seq], r["sr"].at[row_, 0]).start()

    def exchange_in_sent(row_, src, dst):
        for k in range(1, 8):
            to = rem(seq + k, 8)
            remote(src.at[:, to], dst.at[seq], r["ss"].at[row_, k], r["sr"].at[row_, k], seq_peer(k)).wait_send()

    def exchange_in_wait(row_, src, dst):
        local(src.at[:, seq], dst.at[seq], r["sr"].at[row_, 0]).wait()
        for k in range(1, 8):
            frm = rem(seq + 8 - k, 8)
            remote(src.at[:, frm], dst.at[frm], r["ss"].at[row_, k], r["sr"].at[row_, k], seq_peer(k)).wait_recv()

    def exchange_out(row_, src, dst):
        for k in range(1, 8):
            to = rem(seq + k, 8)
            remote(src.at[to], dst.at[:, seq], r["ss"].at[row_, k], r["sr"].at[row_, k], seq_peer(k)).start()
        local(src.at[seq], dst.at[:, seq], r["sr"].at[row_, 0]).start()

    def exchange_out_wait(row_, src, dst):
        local(src.at[seq], dst.at[:, seq], r["sr"].at[row_, 0]).wait()
        for k in range(1, 8):
            frm = rem(seq + 8 - k, 8)
            remote(src.at[frm], dst.at[:, frm], r["ss"].at[row_, k], r["sr"].at[row_, k], seq_peer(k)).wait()

    SHARE = {1: (core == 1, z, z_peer), 2: (core == 0, x, x_peer), 3: (core == z_lo, x, x_peer)}

    def rows_of(q):
        return pl.ds(9 * q, 9)

    def share_y(slot):
        _, q, _ = SHARE[slot]
        return remote(out_w.at[rows_of(q)], r["wo"].at[slot, rows_of(q)], r["ws"].at[slot, 0], r["wr"].at[slot, 0], y_peer(TO[BACK[slot]]))

    def share_line(slot, k, back):
        _, q, peer = SHARE[slot]
        at = rem(q + 4 - k, 4) if back else q
        piece = r["wo"].at[slot, rows_of(at)]
        return remote(piece, piece, r["ws"].at[slot, k], r["wr"].at[slot, k], peer(k))

    def share_core(slot):
        piece = r["wo"].at[slot, pl.ds(0, 36)]
        return remote(piece, piece, r["ws"].at[0, slot], r["wr"].at[0, slot], core_peer())

    def share_start():
        for slot in (1, 2, 3):
            @pl.when(SHARE[slot][0])
            def _(slot=slot):
                share_y(slot).start()

    def share_second():
        for slot in (1, 2, 3):
            @pl.when(SHARE[slot][0])
            def _(slot=slot):
                share_y(slot).wait_recv()
                for k in (2, 1, 3):
                    share_line(slot, k, False).start()

    def share_third():
        for slot in (1, 2, 3):
            @pl.when(SHARE[slot][0])
            def _(slot=slot):
                for k in (1, 2, 3):
                    share_line(slot, k, True).wait_recv()
                share_core(slot).start()

    def share_wait():
        for slot in (1, 2, 3):
            @pl.when(jnp.logical_not(SHARE[slot][0]))
            def _(slot=slot):
                share_core(slot).wait_recv()

    def share_sent():
        for slot in (1, 2, 3):
            @pl.when(SHARE[slot][0])
            def _(slot=slot):
                share_y(slot).wait_send()
                for k in (1, 2, 3):
                    share_line(slot, k, False).wait_send()
                share_core(slot).wait_send()

    def row(i):
        return mod[i]

    def halves(ref, h):
        return ref[4 * h : 4 * h + 4].astype(F32).reshape(64, D)

    lane = lax.broadcasted_iota(jnp.int32, (128, WP), 1)
    head_masks = [(lane >= HEAD_DIM * h) & (lane < HEAD_DIM * (h + 1)) for h in range(HEADS)]
    same_pixel = rem(lax.broadcasted_iota(jnp.int32, (512, 128), 0), 8) == rem(lax.broadcasted_iota(jnp.int32, (512, 128), 1), 8)

    def stacked(v):
        zero = jnp.zeros_like(v)
        return jnp.concatenate([jnp.where(m, v, zero) for m in head_masks], axis=0)

    def side_by_side(v):
        return jnp.concatenate([v[128 * h : 128 * h + 128] for h in range(HEADS)], axis=1)

    def columns(n):
        return pl.ds(pl.multiple_of(n * 384, 384), 384)

    exchange_in(0, lat, r["xs"])
    share_start()
    gather_start(1, r["cy"], PARTS_C, cot, (0, 2))
    for c in weights:
        c.start()
    for j in range(3):
        r["win"][j, W:] = jnp.zeros((WP - W, D), BF16)
    for k in range(4):
        r["wo"][k, 36:] = jnp.zeros((12, 8, D), BF16)
    r["dqc"][:, :, 768:] = jnp.zeros((4, 128, 128), BF16)

    exchange_in_wait(0, lat, r["xs"])
    for h in range(2):
        normed, _ = norm(halves(r["xs"], h))
        r["f"][0, 64 * h : 64 * h + 64, :] = (normed * (1.0 + row(1)) + row(0)).astype(BF16)
    gather_start(0, r["f"], PARTS_T)
    share_second()
    exchange_in(3, cot, r["cg"].at[0])
    for c in weights[:4]:
        c.wait()

    def attend(lo, n):
        block = r["f"][lo : lo + n].reshape(n * 128, D)
        for j in range(3):
            r["qkv"][lo : lo + n, :, j * WP : (j + 1) * WP] = dot(block, r["win"][j], NT).astype(BF16).reshape(n, 128, WP)
        for t in range(lo, lo + n):
            q, kk, v = (r["qkv"][t, :, j * WP : (j + 1) * WP] for j in range(3))
            scores = dot(stacked(q), kk, NT) * SCALE
            scores = jnp.where(same_pixel, scores, -1e30)
            raised = jnp.exp(scores - jnp.max(scores, axis=-1, keepdims=True))
            probs = raised / jnp.sum(raised, axis=-1, keepdims=True)
            r["probs"][t] = probs
            att = dot(side_by_side(probs.astype(BF16)), stacked(v), NN).astype(BF16)
            if t == 0:
                r["at"][0] = att
            else:
                r["as"][t] = att
                part(2, r["as"], r["at"], t).start()

    attend(0, 1)
    gather_pass(0, r["f"], PARTS_T)
    gather_start(1, r["cy"], PARTS_C, cot, (1, 3))
    gather_near(0, r["f"], PARTS_T)
    attend(1, 2)
    share_third()
    gather_far(0, r["f"], PARTS_T)
    attend(3, 1)
    gather_pass(1, r["cy"], PARTS_C)
    gather_near(1, r["cy"], PARTS_C)
    exchange_in(1, r["cy"].at[1], r["cg"].at[1])
    exchange_in(2, r["cy"].at[2], r["cg"].at[2])

    def branch_block(k, row_, src):
        exchange_in_wait(row_, src, r["cg"].at[k])
        for h in range(2):
            r["g"][k, 64 * h : 64 * h + 64, :] = (row(5) * r["cg"][k, 4 * h : 4 * h + 4].astype(F32).reshape(64, D)).astype(BF16)

    def branch_back(lo, m):
        def step(n, c):
            block = r["g"][lo : lo + m].reshape(m * 128, D)
            r["ag"][lo : lo + m, :, columns(n)] = dot(block, r["wdown"][columns(n), :], NT).reshape(m, 128, 384)
            return c

        lax.fori_loop(0, 3, step, 0)

    share_wait()
    part_wait(2, r["as"], r["at"])

    attended = jnp.concatenate([r["at"][k] for k in range(4)], axis=1)
    for n in range(3):
        cols = slice(n * 384, n * 384 + 384)
        r["mid"][:, cols] = dot(attended, r["wo"][:, :, :, cols].reshape(4 * WP, 384), NN)
    for h in range(2):
        rows = slice(64 * h, 64 * h + 64)
        midway = halves(r["xs"], h) + row(2) * r["mid"][rows, :]
        r["mid"][rows, :] = midway
        normed, _ = norm(midway)
        r["s"][0, rows, :] = (normed * (1.0 + row(4)) + row(3)).astype(BF16)
    gather_start(3, r["s"], PARTS_T)

    def mlp(lo, m):
        def hidden_cols(n, c):
            v = dot(r["s"][lo : lo + m].reshape(m * 128, D), r["wup"][:, columns(n)], NN)
            ag = r["ag"][lo : lo + m, :, columns(n)].reshape(m * 128, 384)
            th = jnp.tanh(GELU_C * (v + 0.044715 * (v * v * v)))
            r["act"][lo : lo + m, :, columns(n)] = (0.5 * v * (1.0 + th)).astype(BF16).reshape(m, 128, 384)
            slope = 0.5 * (1.0 + th) + (0.5 * v) * ((1.0 - th * th) * (GELU_C * (1.0 + (3.0 * 0.044715) * (v * v))))
            r["hg"][lo : lo + m, :, columns(n)] = (ag * slope).astype(BF16).reshape(m, 128, 384)
            return c

        lax.fori_loop(0, 3, hidden_cols, 0)

        def grad_cols(n, c):
            out = dot(r["hg"][lo : lo + m].reshape(m * 128, D), r["wup"][columns(n), :], NT)
            r["p5"][lo : lo + m, :, columns(n)] = out.astype(BF16).reshape(m, 128, 384)
            return c

        lax.fori_loop(0, 3, grad_cols, 0)
        for t in range(max(lo, 1), lo + m):
            part(4, r["p5"], r["r5"], t).start()

    branch_block(0, 3, cot)
    weights[4].wait()
    weights[5].wait()
    branch_block(1, 1, r["cy"].at[1])
    branch_block(2, 2, r["cy"].at[2])
    branch_back(0, 3)
    gather_far(1, r["cy"], PARTS_C)
    exchange_in(4, r["cy"].at[3], r["cg"].at[3])
    gather_pass(3, r["s"], PARTS_T)
    mlp(0, 1)
    for k in range(4):
        r["attc"][:, W * k : W * k + W] = r["at"][k, :, :W]
    gather_near(3, r["s"], PARTS_T)
    mlp(1, 2)
    branch_block(3, 4, r["cy"].at[3])
    branch_back(3, 1)
    gather_far(3, r["s"], PARTS_T)
    mlp(3, 1)

    def weight_grad(left_of, right_of, width, *targets):
        def rows_step(m, c):
            out = dot(left_of(columns(m)), right_of(), TN).astype(BF16).reshape(48, 8, width)
            for q in range(16):
                grp = m * 16 + q
                outer = div(grp, 3)
                for name, at, size in targets:
                    to = r["G" + name].at[div(outer, 8), rem(div(outer, 4), 2), rem(outer, 4), pl.ds(rem(grp, 3) * 3, 3)]
                    to[...] = out[3 * q : 3 * q + 3, :, at : at + size]
            return c

        lax.fori_loop(0, 3, rows_step, 0)

    def every(name):
        return lambda cols: r[name][:, :, cols].reshape(512, 384)

    def job_core(index, start):
        name, n, _ = JOBS[index]
        c = remote(r["G" + name].at[:, 1 - core], r["A" + name], r["js"].at[index, 0], r["jr"].at[index, 0], core_peer())
        if start:
            c.start()
        else:
            c.wait()

    def job_core_sum(index):
        name, n, _ = JOBS[index]

        def step(i, c):
            a, b = div(i, 4), rem(i, 4)
            total = r["A" + name][a, b].astype(F32) + r["G" + name][a, core, b].astype(F32)
            r["A" + name][a, b] = total.astype(BF16)
            return c

        lax.fori_loop(0, 8, step, 0)

    def job_first(index, start):
        name, n, x_first = JOBS[index]
        for k in (2, 1, 3):
            if x_first:
                src = r["A" + name].at[:, rem(x + k, 4)]
                where = x_peer(k)
            else:
                other = rem(z + k, 4)
                src = r["A" + name].at[rem(other, 2), :, pl.ds(4 * div(other, 2), 5)]
                where = z_peer(k)
            c = remote(src, r["B" + name].at[k - 1], r["js"].at[index, k], r["jr"].at[index, k], where)
            if start:
                c.start()
            else:
                c.wait()

    def job_first_sum(index):
        name, n, x_first = JOBS[index]
        for a in range(2 if x_first else 4):
            mine = r["A" + name][a, x] if x_first else r["A" + name][z_lo, a, pl.ds(4 * z_hi, 5)]
            total = mine.astype(F32)
            for k in range(3):
                total = total + r["B" + name][k, a].astype(F32)
            r["H" + name][a] = total.astype(BF16)

    def job_second(index, start):
        name, n, x_first = JOBS[index]
        for k in (2, 1, 3):
            if x_first:
                other = rem(z + k, 4)
                src = r["H" + name].at[rem(other, 2), pl.ds(4 * div(other, 2), 5)]
                where = z_peer(k)
            else:
                src = r["H" + name].at[rem(x + k, 4)]
                where = x_peer(k)
            c = remote(src, r["C" + name].at[k - 1], r["js"].at[index, 3 + k], r["jr"].at[index, 3 + k], where)
            if start:
                c.start()
            else:
                c.wait()

    def job_second_sum(index):
        name, n, x_first = JOBS[index]
        mine = r["H" + name][z_lo, pl.ds(4 * z_hi, 5)] if x_first else r["H" + name][x]
        total = mine.astype(F32)
        for k in range(3):
            total = total + r["C" + name][k].astype(F32)
        total = total.reshape(40, n)
        return jnp.where(z_hi == 0, total[:36], total[4:])

    def core_step(index):
        job_core(index, False)
        job_core_sum(index)
        job_first(index, True)

    def first_step(index):
        job_first(index, False)
        job_first_sum(index)
        job_second(index, True)

    weight_grad(every("s"), lambda: r["hg"][...].reshape(512, D), D, ("u", 0, D))
    job_core(0, True)
    weight_grad(every("g"), lambda: r["act"][...].reshape(512, D), D, ("d", 0, D))
    job_core(1, True)
    core_step(0)
    core_step(1)

    part_wait(4, r["p5"], r["r5"])
    for h in range(2):
        rows = slice(64 * h, 64 * h + 64)
        normed, inverse = norm(r["mid"][rows, :])
        back = norm_back(normed, inverse, part_sum(r["p5"], r["r5"], h) * (1.0 + row(4)))
        mg = halves(r["cg"].at[0], h) + back
        r["mg"][rows, :] = mg
        r["ao"][rows, :] = (row(2) * mg).astype(BF16)
    for k in (3, 1, 2, 0):
        grad = dot(r["ao"][...], r["wo"][k].reshape(WP, D), NT).astype(BF16)
        if k:
            r["ds"][k] = grad
            part(5, r["ds"], r["da"], k).start()
        else:
            r["da"][0] = grad
    weight_grad(lambda cols: r["ao"][:, cols], lambda: r["attc"][...], D, ("o", 0, 640), ("p", 640, 512))
    job_core(2, True)
    job_core(3, True)
    part_send_wait(4, r["p5"], r["r5"])

    def result_cols(n, c):
        out = dot(r["act"][...].reshape(512, D), r["wdown"][:, columns(n)], NN)
        r["p5"][:, :, columns(n)] = out.astype(BF16).reshape(4, 128, 384)
        return c

    lax.fori_loop(0, 3, result_cols, 0)
    part(7, r["p5"], r["r8"], 1).start()
    part(7, r["p5"], r["r8"], 2).start()

    def attend_back(lo, m):
        for t in range(lo, lo + m):
            q, kk, v = (r["qkv"][t, :, j * WP : (j + 1) * WP] for j in range(3))
            qs, gs = stacked(q), stacked(r["da"][t])
            probs = r["probs"][t]
            dv = dot(probs.astype(BF16), gs, TN)
            dp_ = dot(gs, v, NT)
            ds = (probs * (dp_ - jnp.sum(probs * dp_, axis=-1, keepdims=True)) * SCALE).astype(BF16)
            dq = dot(side_by_side(ds), stacked(kk), NN)
            dk = dot(ds, qs, TN)
            for j, piece in enumerate((dq, dk, dv)):
                piece = piece.astype(BF16)
                r["dqkv"][t, :, j * WP : (j + 1) * WP] = piece
                r["dqc"][t, :, j * W : (j + 1) * W] = piece[:, :W]
        for n in range(3):
            cols = slice(n * 384, n * 384 + 384)
            total = dot(r["dqkv"][lo : lo + m].reshape(m * 128, D), r["win"][:, :, cols].reshape(D, 384), NN)
            r["p7"][lo : lo + m, :, cols] = total.astype(BF16).reshape(m, 128, 384)
        for t in range(max(lo, 1), lo + m):
            part(6, r["p7"], r["r7"], t).start()

    attend_back(0, 1)
    core_step(2)
    core_step(3)
    part_wait(5, r["ds"], r["da"], (1, 2))
    attend_back(1, 2)
    part_wait(5, r["ds"], r["da"], (3,))
    attend_back(3, 1)

    weight_grad(every("f"), lambda: r["dqc"][...].reshape(512, CI), CI, ("i", 0, 512), ("v", 512, 384))
    job_core(4, True)
    job_core(5, True)
    first_step(0)
    first_step(1)
    core_step(4)
    core_step(5)
    first_step(2)
    first_step(3)

    part_wait(6, r["p7"], r["r7"])
    part(7, r["p5"], r["r8"], 3).start()
    for h in range(2):
        rows = slice(64 * h, 64 * h + 64)
        normed, inverse = norm(halves(r["xs"], h))
        back = norm_back(normed, inverse, part_sum(r["p7"], r["r7"], h) * (1.0 + row(1)))
        out = r["mg"][rows, :] + back
        r["lo"][4 * h : 4 * h + 4] = out.astype(BF16).reshape(4, 2, 8, D)
    exchange_out(6, r["lo"], r["ll"])
    for index, out in ((0, gu), (1, gd)):
        job_second(index, False)
        out[...] = job_second_sum(index).astype(BF16)
    job_second(2, False)
    job_second(3, False)
    both = jnp.concatenate([job_second_sum(2), job_second_sum(3)], axis=1)
    for k in range(4):
        r["oy"][k, :36, :W] = both[:, W * k : W * k + W].astype(BF16)
    for k in (3, 1, 2):
        part(8, r["oy"], r["or"], k).start()
    first_step(4)
    first_step(5)

    part_wait(7, r["p5"], r["r8"])
    for h in range(2):
        rows = slice(64 * h, 64 * h + 64)
        out = r["mid"][rows, :] + row(5) * part_sum(r["p5"], r["r8"], h)
        r["ro"][4 * h : 4 * h + 4] = out.astype(BF16).reshape(4, 2, 8, D)
    exchange_out(5, r["ro"], r["rl"])

    part_wait(8, r["oy"], r["or"])
    total = r["oy"][0, :36, :W].astype(F32)
    for k in (1, 2, 3):
        total = total + r["or"][k, :36, :W].astype(F32)
    go[...] = total.astype(BF16)
    exchange_out_wait(6, r["lo"], r["ll"])
    exchange_out_wait(5, r["ro"], r["rl"])
    done = [local(r["rl"], res, r["osem"].at[0]), local(r["ll"], lgr, r["osem"].at[1])]
    for c in done:
        c.start()
    job_second(4, False)
    job_second(5, False)
    both = jnp.concatenate([job_second_sum(4), job_second_sum(5)], axis=1)
    for j in range(3):
        gi[j] = both[:, W * j : W * j + W].astype(BF16)
    for row_, src, dst in (
        (0, lat, r["xs"]),
        (3, cot, r["cg"].at[0]),
        (1, r["cy"].at[1], r["cg"].at[1]),
        (2, r["cy"].at[2], r["cg"].at[2]),
        (4, r["cy"].at[3], r["cg"].at[3]),
    ):
        exchange_in_sent(row_, src, dst)
    gather_sent(1, r["cy"], PARTS_C, cot)
    gather_sent(0, r["f"], PARTS_T)
    gather_sent(3, r["s"], PARTS_T)
    share_sent()
    for ph, src, dst in ((2, "as", "at"), (5, "ds", "da"), (6, "p7", "r7"), (7, "p5", "r8"), (8, "oy", "or")):
        part_send_wait(ph, r[src], r[dst])
    for c in done:
        c.wait()


def body(latents, modulation, in_weight, out_weight, up_weight, down_weight, cotangent):
    vmem = pl.BlockSpec(memory_space=pltpu.VMEM)
    anywhere = pl.BlockSpec(memory_space=pl.ANY)
    out = lambda *s: jax.ShapeDtypeStruct(s, BF16)
    shapes = (out(2, 8, 8, D), out(2, 8, 8, D), out(36, D), out(36, D), out(3, 36, W), out(36, W))
    found = pl.pallas_call(
        kernel,
        out_shape=shapes,
        in_specs=[anywhere, anywhere, vmem, anywhere, anywhere, anywhere, anywhere],
        out_specs=(anywhere, anywhere, vmem, vmem, vmem, vmem),
        scratch_shapes=list(SPEC.values()),
        compiler_params=pltpu.CompilerParams(collective_id=0, has_side_effects=True, vmem_limit_bytes=67043328),
        name="block",
    )(
        latents.reshape(2, 8, 8, D),
        cotangent.reshape(2, 8, 8, D),
        jnp.transpose(modulation, (1, 0, 2)),
        jnp.transpose(in_weight, (1, 2, 0)),
        out_weight.reshape(36, 8, D),
        up_weight,
        down_weight,
    )
    res, lgr, gu, gd, gi, go = pl.pallas_call(
        hand_over,
        out_shape=shapes,
        in_specs=[anywhere] * 6,
        out_specs=(anywhere,) * 6,
        scratch_shapes=[pltpu.VMEM(v.shape, BF16) for v in shapes] + [pltpu.SemaphoreType.DMA((2, 6))],
        name="hand_over",
    )(*found)
    return (
        res.reshape(latents.shape),
        lgr.reshape(latents.shape),
        jnp.transpose(gi, (1, 0, 2)),
        go.T,
        gu,
        gd.T,
    )


def hand_over(*refs):
    given, outs, held, sems = refs[:6], refs[6:12], refs[12:18], refs[18]
    into = [pltpu.make_async_copy(a, b, sems.at[0, i]) for i, (a, b) in enumerate(zip(given, held))]
    back = [pltpu.make_async_copy(a, b, sems.at[1, i]) for i, (a, b) in enumerate(zip(held, outs))]
    for c in into:
        c.start()
    for c, d in zip(into, back):
        c.wait()
        d.start()
    for d in back:
        d.wait()


def solution(mesh):
    placed = (
        P("dp", "seq", "tensor", None),
        P("dp", None, None),
        P(None, None, "tensor"),
        P("tensor", None),
        P(None, "tensor"),
        P("tensor", None),
        P("dp", "seq", "tensor", None),
    )
    return jax.shard_map(
        body,
        mesh=mesh,
        in_specs=placed,
        out_specs=(
            P("dp", "seq", "tensor", None),
            P("dp", "seq", "tensor", None),
            P(("dp", "seq"), None, "tensor"),
            P("tensor", ("dp", "seq")),
            P(("dp", "seq"), "tensor"),
            P("tensor", ("dp", "seq")),
        ),
        check_vma=False,
    )
```

time: 119 us -> 115 us (0.966)
  Pallas kernels: 118 us -> 114 us
    pallas_call x1, Pallas kernels: 116 us -> 112 us  [body(): pl.pallas_call(kernel, out_shape=shapes, in_specs=[anywhere, anywhere, vm...]
where the time goes in v3:
time: 115 us
  Pallas kernels  114 us (99%)
    pallas_call x1, Pallas kernels, body(): pl.pallas_call(kernel, out_shape=shapes, in_specs=[anywhere, anywhere, vm...  112 us

profile of v3, /device:TPU:0, one launch (start us, length us, event | category | flops | bytes accessed | tf_op | source)
XLA Modules:
  0.0 115.1 jit_solution(2398159016681703686)
XLA Ops:
  0.6 112.3 %block.1 = (bf16[2,8,8,1152]{3,2,1,0:T(8,128)(2,1)}, bf16[2,8,8,1152]{3,2,1,0:T(8,128)(2,1)}, bf16[36,1152]{1,0:T(8,128)(2,1)}, bf16[36,1152]{1,0:T(8,128)(2,1)}...) custom-call(bf16[2,8,8,1152]{3,2,1,0:T(8,128)(2,1)} %bitcast.12, bf16[2,8,8,1152]{3,2,1,0:T(8,128)(2,1)} %bitcast.13, ...), custom_call_target="tpu_custom_call" | custom-call | tf_op jit(solution)/shard_map/block/pallas_call | solution.py:651
  112.9 2.0 %hand_over.1 = (bf16[2,8,8,1152]{3,2,1,0:T(8,128)(2,1)}, bf16[2,8,8,1152]{3,2,1,0:T(8,128)(2,1)}, bf16[36,1152]{1,0:T(8,128)(2,1)}, bf16[36,1152]{1,0:T(8,128)(2...) custom-call(bf16[2,8,8,1152]{3,2,1,0:T(8,128)(2,1)} %get-tuple-element.18.refs_0_, ...), custom_call_target="tpu_custom_call" | custom-call | tf_op jit(solution)/shard_map/hand_over/pallas_call | solution.py:668

commit v4 on v3

--- a/solution.py
+++ b/solution.py
@@ -62,28 +62,30 @@
         "win": vm(3, WP, D), "wo": vm(4, 48, 8, D), "wup": vm(D, D), "wdown": vm(D, D),
         "f": vm(4, 128, D), "s": vm(4, 128, D), "g": vm(4, 128, D), "ao": vm(128, D),
         "p5": vm(4, 128, D), "p7": vm(4, 128, D), "ag": vm(4, 128, D, t=F32),
-        "r5": vm(4, 128, D), "r7": vm(4, 128, D), "r8": vm(4, 128, D),
+        "r5": vm(4, 128, D), "r7": vm(4, 128, D), "p8": vm(4, 128, D), "t8": vm(2, 64, D), "r8": vm(2, 128, D),
         "qkv": vm(4, 128, 3 * WP), "probs": vm(4, 512, 128, t=F32),
         "as": vm(4, 128, WP), "at": vm(4, 128, WP), "ds": vm(4, 128, WP), "da": vm(4, 128, WP), "attc": vm(128, D),
         "act": vm(4, 128, D), "hg": vm(4, 128, D), "dqkv": vm(4, 128, 3 * WP), "dqc": vm(4, 128, CI),
         "mid": vm(128, D, t=F32), "mg": vm(128, D, t=F32),
         "ro": vm(8, 2, 8, D), "lo": vm(8, 2, 8, D), "rl": vm(2, 8, 8, D), "ll": vm(2, 8, 8, D),
         "oy": vm(4, 40, WP), "or": vm(4, 40, WP),
-        "wsem": dma(6),
+        "wsem": dma(7), "mod": vm(6, 1, D, t=F32),
         "ys": dma(10, 6), "yr": dma(10, 6),
         "ss": dma(7, 8), "sr": dma(7, 8),
         "osem": dma(2),
-        "js": dma(6, 7), "jr": dma(6, 7),
+        "js": dma(6, 10), "jr": dma(6, 10),
         "ws": dma(4, 4), "wr": dma(4, 4),
     }
     for name, n, x_first in JOBS:
         spec["G" + name] = vm(2, 2, 4, 9, 8, n)
         spec["A" + name] = vm(2, 4, 9, 8, n)
         if x_first:
-            spec["B" + name] = vm(3, 2, 9, 8, n)
+            spec["B" + name] = vm(2, 2, 9, 8, n)
+            spec["T" + name] = vm(2, 1, 9, 8, n)
             spec["H" + name] = vm(2, 9, 8, n)
         else:
-            spec["B" + name] = vm(3, 4, 5, 8, n)
+            spec["B" + name] = vm(2, 4, 5, 8, n)
+            spec["T" + name] = vm(2, 2, 5, 8, n)
             spec["H" + name] = vm(4, 5, 8, n)
         spec["C" + name] = vm(3, 5, 8, n)
     return spec
@@ -98,7 +100,7 @@
 PARTS_T = (lambda v: v.at[pl.ds(0, 64)], lambda v: v.at[pl.ds(64, 64)])
 
 
-def kernel(lat, cot, mod, in_w, out_w, up_w, down_w, res, lgr, gu, gd, gi, go, *scratch):
+def kernel(lat, cot, mod_in, in_w, out_w, up_w, down_w, res, lgr, gu, gd, gi, go, *scratch):
     r = dict(zip(SPEC, scratch))
     dp, seq, me = lax.axis_index("dp"), lax.axis_index("seq"), lax.axis_index("tensor")
     core, z_lo = rem(dp, 2), div(dp, 2)
@@ -134,6 +136,9 @@
         local(down_w, r["wdown"], r["wsem"].at[5]),
     ]
 
+    mod = r["mod"]
+    mod_copy = local(mod_in, mod, r["wsem"].at[6])
+    mod_copy.start()
     barrier = pltpu.get_barrier_semaphore()
     peers = [seq_peer(k) for k in range(1, 8)] + [y_peer(k) for k in range(1, 4)] + [core_peer()]
     peers += [z_peer(1), z_peer(3)]
@@ -302,6 +307,7 @@
         r["wo"][k, 36:] = jnp.zeros((12, 8, D), BF16)
     r["dqc"][:, :, 768:] = jnp.zeros((4, 128, 128), BF16)
 
+    mod_copy.wait()
     exchange_in_wait(0, lat, r["xs"])
     for h in range(2):
         normed, _ = norm(halves(r["xs"], h))
@@ -370,6 +376,8 @@
         normed, _ = norm(midway)
         r["s"][0, rows, :] = (normed * (1.0 + row(4)) + row(3)).astype(BF16)
     gather_start(3, r["s"], PARTS_T)
+    gather_far(1, r["cy"], PARTS_C)
+    exchange_in(4, r["cy"].at[3], r["cg"].at[3])
 
     def mlp(lo, m):
         def hidden_cols(n, c):
@@ -398,8 +406,6 @@
     branch_block(1, 1, r["cy"].at[1])
     branch_block(2, 2, r["cy"].at[2])
     branch_back(0, 3)
-    gather_far(1, r["cy"], PARTS_C)
-    exchange_in(4, r["cy"].at[3], r["cg"].at[3])
     gather_pass(3, r["s"], PARTS_T)
     mlp(0, 1)
     for k in range(4):
@@ -446,28 +452,62 @@
 
         lax.fori_loop(0, 8, step, 0)
 
+    def ring(index):
+        name, n, x_first = JOBS[index]
+        half = 1 if x_first else 2
+
+        def piece(k, h):
+            part_of = pl.ds(h * half, half)
+            if x_first:
+                return r["A" + name].at[part_of, rem(x + k, 4)]
+            at = rem(z + k, 4)
+            return r["A" + name].at[rem(at, 2), part_of, pl.ds(4 * div(at, 2), 5)]
+
+        def send(src, dst, m, k):
+            return remote(src, dst, r["js"].at[index, m], r["jr"].at[index, m], (x_peer if x_first else z_peer)(k))
+
+        through, landed = r["T" + name], r["B" + name]
+        first, last = pl.ds(0, half), pl.ds(half, half)
+
+        def copy(m):
+            src, dst, k = (
+                (piece(2, 0), through.at[0], 1),
+                (piece(2, 1), through.at[1], 3),
+                (piece(1, 1), landed.at[0, last], 1),
+                (piece(3, 0), landed.at[1, first], 3),
+                (through.at[0], landed.at[0, first], 1),
+                (through.at[1], landed.at[1, last], 3),
+            )[m]
+            return send(src, dst, m + 1, k)
+
+        return piece, copy
+
     def job_first(index, start):
-        name, n, x_first = JOBS[index]
-        for k in (2, 1, 3):
-            if x_first:
-                src = r["A" + name].at[:, rem(x + k, 4)]
-                where = x_peer(k)
-            else:
-                other = rem(z + k, 4)
-                src = r["A" + name].at[rem(other, 2), :, pl.ds(4 * div(other, 2), 5)]
-                where = z_peer(k)
-            c = remote(src, r["B" + name].at[k - 1], r["js"].at[index, k], r["jr"].at[index, k], where)
-            if start:
-                c.start()
-            else:
-                c.wait()
+        _, copy = ring(index)
+        if start:
+            for m in range(4):
+                copy(m).start()
+        else:
+            for m in range(2):
+                copy(m).wait_send()
+            for m in range(2, 6):
+                copy(m).wait()
+
+    def relay(index):
+        name = JOBS[index][0]
+        piece, copy = ring(index)
+        for h, k in ((0, 1), (1, 3)):
+            copy(h).wait_recv()
+            total = r["T" + name][h].astype(F32) + piece(k, h)[...].astype(F32)
+            r["T" + name][h] = total.astype(BF16)
+            copy(4 + h).start()
 
     def job_first_sum(index):
         name, n, x_first = JOBS[index]
         for a in range(2 if x_first else 4):
             mine = r["A" + name][a, x] if x_first else r["A" + name][z_lo, a, pl.ds(4 * z_hi, 5)]
             total = mine.astype(F32)
-            for k in range(3):
+            for k in range(2):
                 total = total + r["B" + name][k, a].astype(F32)
             r["H" + name][a] = total.astype(BF16)
 
@@ -481,7 +521,7 @@
             else:
                 src = r["H" + name].at[rem(x + k, 4)]
                 where = x_peer(k)
-            c = remote(src, r["C" + name].at[k - 1], r["js"].at[index, 3 + k], r["jr"].at[index, 3 + k], where)
+            c = remote(src, r["C" + name].at[k - 1], r["js"].at[index, 6 + k], r["jr"].at[index, 6 + k], where)
             if start:
                 c.start()
             else:
@@ -510,6 +550,27 @@
     job_core(0, True)
     weight_grad(every("g"), lambda: r["act"][...].reshape(512, D), D, ("d", 0, D))
     job_core(1, True)
+
+    def result_cols(n, c):
+        out = dot(r["act"][...].reshape(512, D), r["wdown"][:, columns(n)], NN)
+        r["p8"][:, :, columns(n)] = out.astype(BF16).reshape(4, 128, 384)
+        return c
+
+    lax.fori_loop(0, 3, result_cols, 0)
+
+    low, high = pl.ds(0, 64), pl.ds(64, 64)
+
+    def result_part(m):
+        src, dst, to = (
+            (r["p8"].at[3, low], r["t8"].at[0], 1),
+            (r["p8"].at[3, high], r["t8"].at[1], 3),
+            (r["p8"].at[2, high], r["r8"].at[0, high], 1),
+            (r["p8"].at[1, low], r["r8"].at[1, low], 3),
+            (r["t8"].at[0], r["r8"].at[0, low], 1),
+            (r["t8"].at[1], r["r8"].at[1, high], 3),
+        )[m]
+        return remote(src, dst, r["ys"].at[7, m], r["yr"].at[7, m], y_peer(to))
+
     core_step(0)
     core_step(1)
 
@@ -528,20 +589,13 @@
             part(5, r["ds"], r["da"], k).start()
         else:
             r["da"][0] = grad
+    for m in range(4):
+        result_part(m).start()
     weight_grad(lambda cols: r["ao"][:, cols], lambda: r["attc"][...], D, ("o", 0, 640), ("p", 640, 512))
     job_core(2, True)
     job_core(3, True)
-    part_send_wait(4, r["p5"], r["r5"])
-
-    def result_cols(n, c):
-        out = dot(r["act"][...].reshape(512, D), r["wdown"][:, columns(n)], NN)
-        r["p5"][:, :, columns(n)] = out.astype(BF16).reshape(4, 128, 384)
-        return c
-
-    lax.fori_loop(0, 3, result_cols, 0)
-    part(7, r["p5"], r["r8"], 1).start()
-    part(7, r["p5"], r["r8"], 2).start()
-
+    relay(0)
+    relay(1)
     def attend_back(lo, m):
         for t in range(lo, lo + m):
             q, kk, v = (r["qkv"][t, :, j * WP : (j + 1) * WP] for j in range(3))
@@ -574,15 +628,23 @@
     weight_grad(every("f"), lambda: r["dqc"][...].reshape(512, CI), CI, ("i", 0, 512), ("v", 512, 384))
     job_core(4, True)
     job_core(5, True)
+    relay(2)
+    relay(3)
     first_step(0)
     first_step(1)
+    for m in range(2):
+        result_part(m).wait_recv()
+        mine = r["p8"][2, 0:64] if m == 0 else r["p8"][1, 64:128]
+        r["t8"][m] = (r["t8"][m].astype(F32) + mine.astype(F32)).astype(BF16)
+        result_part(4 + m).start()
     core_step(4)
     core_step(5)
     first_step(2)
     first_step(3)
+    relay(4)
+    relay(5)
 
     part_wait(6, r["p7"], r["r7"])
-    part(7, r["p5"], r["r8"], 3).start()
     for h in range(2):
         rows = slice(64 * h, 64 * h + 64)
         normed, inverse = norm(halves(r["xs"], h))
@@ -603,10 +665,12 @@
     first_step(4)
     first_step(5)
 
-    part_wait(7, r["p5"], r["r8"])
+    for m in range(2, 6):
+        result_part(m).wait_recv()
     for h in range(2):
         rows = slice(64 * h, 64 * h + 64)
-        out = r["mid"][rows, :] + row(5) * part_sum(r["p5"], r["r8"], h)
+        total = r["p8"][0, rows, :].astype(F32) + r["r8"][0, rows, :].astype(F32) + r["r8"][1, rows, :].astype(F32)
+        out = r["mid"][rows, :] + row(5) * total
         r["ro"][4 * h : 4 * h + 4] = out.astype(BF16).reshape(4, 2, 8, D)
     exchange_out(5, r["ro"], r["rl"])
 
@@ -637,7 +701,9 @@
     gather_sent(0, r["f"], PARTS_T)
     gather_sent(3, r["s"], PARTS_T)
     share_sent()
-    for ph, src, dst in ((2, "as", "at"), (5, "ds", "da"), (6, "p7", "r7"), (7, "p5", "r8"), (8, "oy", "or")):
+    for m in range(6):
+        result_part(m).wait_send()
+    for ph, src, dst in ((2, "as", "at"), (5, "ds", "da"), (6, "p7", "r7"), (4, "p5", "r5"), (8, "oy", "or")):
         part_send_wait(ph, r[src], r[dst])
     for c in done:
         c.wait()
@@ -651,7 +717,7 @@
     found = pl.pallas_call(
         kernel,
         out_shape=shapes,
-        in_specs=[anywhere, anywhere, vmem, anywhere, anywhere, anywhere, anywhere],
+        in_specs=[anywhere] * 7,
         out_specs=(anywhere, anywhere, vmem, vmem, vmem, vmem),
         scratch_shapes=list(SPEC.values()),
         compiler_params=pltpu.CompilerParams(collective_id=0, has_side_effects=True, vmem_limit_bytes=67043328),

time: 115 us -> 111 us (0.965)
  Pallas kernels: 114 us -> 110 us
    pallas_call x1, Pallas kernels: 112 us -> 108 us  [body(): pl.pallas_call(kernel, out_shape=shapes, in_specs=[anywhere] * 7, out_spe...]
where the time goes in v4:
time: 111 us
  Pallas kernels  110 us (99%)
    pallas_call x1, Pallas kernels, body(): pl.pallas_call(kernel, out_shape=shapes, in_specs=[anywhere] * 7, out_spe...  108 us

profile of v4, /device:TPU:0, one launch (start us, length us, event | category | flops | bytes accessed | tf_op | source)
XLA Modules:
  0.0 110.6 jit_solution(18036862004885022939)
XLA Ops:
  0.6 107.8 %block.1 = (bf16[2,8,8,1152]{3,2,1,0:T(8,128)(2,1)}, bf16[2,8,8,1152]{3,2,1,0:T(8,128)(2,1)}, bf16[36,1152]{1,0:T(8,128)(2,1)}, bf16[36,1152]{1,0:T(8,128)(2,1)}...) custom-call(bf16[2,8,8,1152]{3,2,1,0:T(8,128)(2,1)} %bitcast.12, bf16[2,8,8,1152]{3,2,1,0:T(8,128)(2,1)} %bitcast.13, ...), custom_call_target="tpu_custom_call" | custom-call | tf_op jit(solution)/shard_map/block/pallas_call | solution.py:717
  108.4 2.0 %hand_over.1 = (bf16[2,8,8,1152]{3,2,1,0:T(8,128)(2,1)}, bf16[2,8,8,1152]{3,2,1,0:T(8,128)(2,1)}, bf16[36,1152]{1,0:T(8,128)(2,1)}, bf16[36,1152]{1,0:T(8,128)(2...) custom-call(bf16[2,8,8,1152]{3,2,1,0:T(8,128)(2,1)} %get-tuple-element.18.refs_0_, ...), custom_call_target="tpu_custom_call" | custom-call | tf_op jit(solution)/shard_map/hand_over/pallas_call | solution.py:734

commit v5 on v4

--- a/solution.py
+++ b/solution.py
@@ -62,7 +62,7 @@
         "win": vm(3, WP, D), "wo": vm(4, 48, 8, D), "wup": vm(D, D), "wdown": vm(D, D),
         "f": vm(4, 128, D), "s": vm(4, 128, D), "g": vm(4, 128, D), "ao": vm(128, D),
         "p5": vm(4, 128, D), "p7": vm(4, 128, D), "ag": vm(4, 128, D, t=F32),
-        "r5": vm(4, 128, D), "r7": vm(4, 128, D), "p8": vm(4, 128, D), "t8": vm(2, 64, D), "r8": vm(2, 128, D),
+        "r5": vm(4, 128, D), "t7": vm(2, 64, D), "r7": vm(2, 128, D), "p8": vm(4, 128, D), "t8": vm(2, 64, D), "r8": vm(2, 128, D),
         "qkv": vm(4, 128, 3 * WP), "probs": vm(4, 512, 128, t=F32),
         "as": vm(4, 128, WP), "at": vm(4, 128, WP), "ds": vm(4, 128, WP), "da": vm(4, 128, WP), "attc": vm(128, D),
         "act": vm(4, 128, D), "hg": vm(4, 128, D), "dqkv": vm(4, 128, 3 * WP), "dqc": vm(4, 128, CI),
@@ -299,7 +299,7 @@
     exchange_in(0, lat, r["xs"])
     share_start()
     gather_start(1, r["cy"], PARTS_C, cot, (0, 2))
-    for c in weights:
+    for c in weights[:4]:
         c.start()
     for j in range(3):
         r["win"][j, W:] = jnp.zeros((WP - W, D), BF16)
@@ -313,6 +313,8 @@
         normed, _ = norm(halves(r["xs"], h))
         r["f"][0, 64 * h : 64 * h + 64, :] = (normed * (1.0 + row(1)) + row(0)).astype(BF16)
     gather_start(0, r["f"], PARTS_T)
+    for c in weights[4:]:
+        c.start()
     share_second()
     exchange_in(3, cot, r["cg"].at[0])
     for c in weights[:4]:
@@ -362,6 +364,10 @@
 
         lax.fori_loop(0, 3, step, 0)
 
+    branch_block(0, 3, cot)
+    weights[4].wait()
+    weights[5].wait()
+    branch_back(0, 1)
     share_wait()
     part_wait(2, r["as"], r["at"])
 
@@ -400,16 +406,13 @@
         for t in range(max(lo, 1), lo + m):
             part(4, r["p5"], r["r5"], t).start()
 
-    branch_block(0, 3, cot)
-    weights[4].wait()
-    weights[5].wait()
-    branch_block(1, 1, r["cy"].at[1])
-    branch_block(2, 2, r["cy"].at[2])
-    branch_back(0, 3)
-    gather_pass(3, r["s"], PARTS_T)
     mlp(0, 1)
     for k in range(4):
         r["attc"][:, W * k : W * k + W] = r["at"][k, :, :W]
+    gather_pass(3, r["s"], PARTS_T)
+    branch_block(1, 1, r["cy"].at[1])
+    branch_block(2, 2, r["cy"].at[2])
+    branch_back(1, 2)
     gather_near(3, r["s"], PARTS_T)
     mlp(1, 2)
     branch_block(3, 4, r["cy"].at[3])
@@ -560,16 +563,34 @@
 
     low, high = pl.ds(0, 64), pl.ds(64, 64)
 
-    def result_part(m):
+    def halved(ph, p, t, q, m):
         src, dst, to = (
-            (r["p8"].at[3, low], r["t8"].at[0], 1),
-            (r["p8"].at[3, high], r["t8"].at[1], 3),
-            (r["p8"].at[2, high], r["r8"].at[0, high], 1),
-            (r["p8"].at[1, low], r["r8"].at[1, low], 3),
-            (r["t8"].at[0], r["r8"].at[0, low], 1),
-            (r["t8"].at[1], r["r8"].at[1, high], 3),
+            (r[p].at[3, low], r[t].at[0], 1),
+            (r[p].at[3, high], r[t].at[1], 3),
+            (r[p].at[2, high], r[q].at[0, high], 1),
+            (r[p].at[1, low], r[q].at[1, low], 3),
+            (r[t].at[0], r[q].at[0, low], 1),
+            (r[t].at[1], r[q].at[1, high], 3),
         )[m]
-        return remote(src, dst, r["ys"].at[7, m], r["yr"].at[7, m], y_peer(to))
+        return remote(src, dst, r["ys"].at[ph, m], r["yr"].at[ph, m], y_peer(to))
+
+    def halved_relay(ph, p, t, q):
+        for m in range(2):
+            halved(ph, p, t, q, m).wait_recv()
+            mine = r[p][2, 0:64] if m == 0 else r[p][1, 64:128]
+            r[t][m] = (r[t][m].astype(F32) + mine.astype(F32)).astype(BF16)
+            halved(ph, p, t, q, 4 + m).start()
+
+    def halved_wait(ph, p, t, q):
+        for m in range(2, 6):
+            halved(ph, p, t, q, m).wait_recv()
+
+    def halved_sum(p, q, h):
+        rows = slice(64 * h, 64 * h + 64)
+        return r[p][0, rows, :].astype(F32) + r[q][0, rows, :].astype(F32) + r[q][1, rows, :].astype(F32)
+
+    RESULT = (7, "p8", "t8", "r8")
+    INPUT = (6, "p7", "t7", "r7")
 
     core_step(0)
     core_step(1)
@@ -590,7 +611,7 @@
         else:
             r["da"][0] = grad
     for m in range(4):
-        result_part(m).start()
+        halved(*RESULT, m).start()
     weight_grad(lambda cols: r["ao"][:, cols], lambda: r["attc"][...], D, ("o", 0, 640), ("p", 640, 512))
     job_core(2, True)
     job_core(3, True)
@@ -614,44 +635,51 @@
             cols = slice(n * 384, n * 384 + 384)
             total = dot(r["dqkv"][lo : lo + m].reshape(m * 128, D), r["win"][:, :, cols].reshape(D, 384), NN)
             r["p7"][lo : lo + m, :, cols] = total.astype(BF16).reshape(m, 128, 384)
-        for t in range(max(lo, 1), lo + m):
-            part(6, r["p7"], r["r7"], t).start()
 
     attend_back(0, 1)
     core_step(2)
     core_step(3)
+    part_wait(5, r["ds"], r["da"], (3,))
+    attend_back(3, 1)
+    halved(*INPUT, 0).start()
+    halved(*INPUT, 1).start()
     part_wait(5, r["ds"], r["da"], (1, 2))
     attend_back(1, 2)
-    part_wait(5, r["ds"], r["da"], (3,))
-    attend_back(3, 1)
+    halved(*INPUT, 2).start()
+    halved(*INPUT, 3).start()
 
     weight_grad(every("f"), lambda: r["dqc"][...].reshape(512, CI), CI, ("i", 0, 512), ("v", 512, 384))
     job_core(4, True)
     job_core(5, True)
+    halved_relay(*INPUT)
+    halved_relay(*RESULT)
     relay(2)
     relay(3)
     first_step(0)
     first_step(1)
-    for m in range(2):
-        result_part(m).wait_recv()
-        mine = r["p8"][2, 0:64] if m == 0 else r["p8"][1, 64:128]
-        r["t8"][m] = (r["t8"][m].astype(F32) + mine.astype(F32)).astype(BF16)
-        result_part(4 + m).start()
     core_step(4)
     core_step(5)
+    halved_wait(*INPUT)
+    for h in range(2):
+        rows = slice(64 * h, 64 * h + 64)
+        normed, inverse = norm(halves(r["xs"], h))
+        back = norm_back(normed, inverse, halved_sum("p7", "r7", h) * (1.0 + row(1)))
+        out = r["mg"][rows, :] + back
+        r["lo"][4 * h : 4 * h + 4] = out.astype(BF16).reshape(4, 2, 8, D)
+    exchange_out(6, r["lo"], r["ll"])
     first_step(2)
     first_step(3)
     relay(4)
     relay(5)
 
-    part_wait(6, r["p7"], r["r7"])
+    halved_wait(*RESULT)
     for h in range(2):
         rows = slice(64 * h, 64 * h + 64)
-        normed, inverse = norm(halves(r["xs"], h))
-        back = norm_back(normed, inverse, part_sum(r["p7"], r["r7"], h) * (1.0 + row(1)))
-        out = r["mg"][rows, :] + back
-        r["lo"][4 * h : 4 * h + 4] = out.astype(BF16).reshape(4, 2, 8, D)
-    exchange_out(6, r["lo"], r["ll"])
+        out = r["mid"][rows, :] + row(5) * halved_sum("p8", "r8", h)
+        r["ro"][4 * h : 4 * h + 4] = out.astype(BF16).reshape(4, 2, 8, D)
+    exchange_out(5, r["ro"], r["rl"])
+
+
     for index, out in ((0, gu), (1, gd)):
         job_second(index, False)
         out[...] = job_second_sum(index).astype(BF16)
@@ -664,15 +692,6 @@
         part(8, r["oy"], r["or"], k).start()
     first_step(4)
     first_step(5)
-
-    for m in range(2, 6):
-        result_part(m).wait_recv()
-    for h in range(2):
-        rows = slice(64 * h, 64 * h + 64)
-        total = r["p8"][0, rows, :].astype(F32) + r["r8"][0, rows, :].astype(F32) + r["r8"][1, rows, :].astype(F32)
-        out = r["mid"][rows, :] + row(5) * total
-        r["ro"][4 * h : 4 * h + 4] = out.astype(BF16).reshape(4, 2, 8, D)
-    exchange_out(5, r["ro"], r["rl"])
 
     part_wait(8, r["oy"], r["or"])
     total = r["oy"][0, :36, :W].astype(F32)
@@ -702,8 +721,9 @@
     gather_sent(3, r["s"], PARTS_T)
     share_sent()
     for m in range(6):
-        result_part(m).wait_send()
-    for ph, src, dst in ((2, "as", "at"), (5, "ds", "da"), (6, "p7", "r7"), (4, "p5", "r5"), (8, "oy", "or")):
+        halved(*RESULT, m).wait_send()
+        halved(*INPUT, m).wait_send()
+    for ph, src, dst in ((2, "as", "at"), (5, "ds", "da"), (4, "p5", "r5"), (8, "oy", "or")):
         part_send_wait(ph, r[src], r[dst])
     for c in done:
         c.wait()

time: 111 us -> 111 us (level)
  no operation moved by 1% of the time
where the time goes in v5:
time: 111 us; the launch traced here: 110 us
  Pallas kernels  110 us (99%)
    pallas_call x1, Pallas kernels, body(): pl.pallas_call(kernel, out_shape=shapes, in_specs=[anywhere] * 7, out_spe...  108 us

profile of v5, /device:TPU:0, one launch (start us, length us, event | category | flops | bytes accessed | tf_op | source)
XLA Modules:
  0.0 110.4 jit_solution(8595784358241758649)
XLA Ops:
  0.6 107.6 %block.1 = (bf16[2,8,8,1152]{3,2,1,0:T(8,128)(2,1)}, bf16[2,8,8,1152]{3,2,1,0:T(8,128)(2,1)}, bf16[36,1152]{1,0:T(8,128)(2,1)}, bf16[36,1152]{1,0:T(8,128)(2,1)}...) custom-call(bf16[2,8,8,1152]{3,2,1,0:T(8,128)(2,1)} %bitcast.12, bf16[2,8,8,1152]{3,2,1,0:T(8,128)(2,1)} %bitcast.13, ...), custom_call_target="tpu_custom_call" | custom-call | tf_op jit(solution)/shard_map/block/pallas_call | solution.py:737
  108.3 2.0 %hand_over.1 = (bf16[2,8,8,1152]{3,2,1,0:T(8,128)(2,1)}, bf16[2,8,8,1152]{3,2,1,0:T(8,128)(2,1)}, bf16[36,1152]{1,0:T(8,128)(2,1)}, bf16[36,1152]{1,0:T(8,128)(2...) custom-call(bf16[2,8,8,1152]{3,2,1,0:T(8,128)(2,1)} %get-tuple-element.18.refs_0_, ...), custom_call_target="tpu_custom_call" | custom-call | tf_op jit(solution)/shard_map/hand_over/pallas_call | solution.py:754

commit v6 on v5

--- a/solution.py
+++ b/solution.py
@@ -554,13 +554,6 @@
     weight_grad(every("g"), lambda: r["act"][...].reshape(512, D), D, ("d", 0, D))
     job_core(1, True)
 
-    def result_cols(n, c):
-        out = dot(r["act"][...].reshape(512, D), r["wdown"][:, columns(n)], NN)
-        r["p8"][:, :, columns(n)] = out.astype(BF16).reshape(4, 128, 384)
-        return c
-
-    lax.fori_loop(0, 3, result_cols, 0)
-
     low, high = pl.ds(0, 64), pl.ds(64, 64)
 
     def halved(ph, p, t, q, m):
@@ -610,7 +603,13 @@
             part(5, r["ds"], r["da"], k).start()
         else:
             r["da"][0] = grad
-    for m in range(4):
+    def result_cols(n, c):
+        out = dot(r["act"][...].reshape(512, D), r["wdown"][:, columns(n)], NN)
+        r["p8"][:, :, columns(n)] = out.astype(BF16).reshape(4, 128, 384)
+        return c
+
+    lax.fori_loop(0, 3, result_cols, 0)
+    for m in range(2):
         halved(*RESULT, m).start()
     weight_grad(lambda cols: r["ao"][:, cols], lambda: r["attc"][...], D, ("o", 0, 640), ("p", 640, 512))
     job_core(2, True)
@@ -652,6 +651,8 @@
     job_core(4, True)
     job_core(5, True)
     halved_relay(*INPUT)
+    for m in (2, 3):
+        halved(*RESULT, m).start()
     halved_relay(*RESULT)
     relay(2)
     relay(3)

time: 111 us -> 110 us (level)
  no operation moved by 1% of the time
where the time goes in v6:
time: 110 us
  Pallas kernels  109 us (99%)
    pallas_call x1, Pallas kernels, body(): pl.pallas_call(kernel, out_shape=shapes, in_specs=[anywhere] * 7, out_spe...  107 us

profile of v6, /device:TPU:0, one launch (start us, length us, event | category | flops | bytes accessed | tf_op | source)
XLA Modules:
  0.0 110.3 jit_solution(4755114090542624619)
XLA Ops:
  0.6 107.5 %block.1 = (bf16[2,8,8,1152]{3,2,1,0:T(8,128)(2,1)}, bf16[2,8,8,1152]{3,2,1,0:T(8,128)(2,1)}, bf16[36,1152]{1,0:T(8,128)(2,1)}, bf16[36,1152]{1,0:T(8,128)(2,1)}...) custom-call(bf16[2,8,8,1152]{3,2,1,0:T(8,128)(2,1)} %bitcast.12, bf16[2,8,8,1152]{3,2,1,0:T(8,128)(2,1)} %bitcast.13, ...), custom_call_target="tpu_custom_call" | custom-call | tf_op jit(solution)/shard_map/block/pallas_call | solution.py:738
  108.1 2.0 %hand_over.1 = (bf16[2,8,8,1152]{3,2,1,0:T(8,128)(2,1)}, bf16[2,8,8,1152]{3,2,1,0:T(8,128)(2,1)}, bf16[36,1152]{1,0:T(8,128)(2,1)}, bf16[36,1152]{1,0:T(8,128)(2...) custom-call(bf16[2,8,8,1152]{3,2,1,0:T(8,128)(2,1)} %get-tuple-element.18.refs_0_, ...), custom_call_target="tpu_custom_call" | custom-call | tf_op jit(solution)/shard_map/hand_over/pallas_call | solution.py:755

commit v7 on v6

--- a/solution.py
+++ b/solution.py
@@ -660,6 +660,9 @@
     first_step(1)
     core_step(4)
     core_step(5)
+    first_step(2)
+    first_step(3)
+
     halved_wait(*INPUT)
     for h in range(2):
         rows = slice(64 * h, 64 * h + 64)
@@ -668,8 +671,6 @@
         out = r["mg"][rows, :] + back
         r["lo"][4 * h : 4 * h + 4] = out.astype(BF16).reshape(4, 2, 8, D)
     exchange_out(6, r["lo"], r["ll"])
-    first_step(2)
-    first_step(3)
     relay(4)
     relay(5)
 
@@ -679,7 +680,6 @@
         out = r["mid"][rows, :] + row(5) * halved_sum("p8", "r8", h)
         r["ro"][4 * h : 4 * h + 4] = out.astype(BF16).reshape(4, 2, 8, D)
     exchange_out(5, r["ro"], r["rl"])
-
 
     for index, out in ((0, gu), (1, gd)):
         job_second(index, False)
@@ -694,16 +694,16 @@
     first_step(4)
     first_step(5)
 
+    done = [local(r["rl"], res, r["osem"].at[0]), local(r["ll"], lgr, r["osem"].at[1])]
+    exchange_out_wait(6, r["lo"], r["ll"])
+    done[1].start()
     part_wait(8, r["oy"], r["or"])
     total = r["oy"][0, :36, :W].astype(F32)
     for k in (1, 2, 3):
         total = total + r["or"][k, :36, :W].astype(F32)
     go[...] = total.astype(BF16)
-    exchange_out_wait(6, r["lo"], r["ll"])
     exchange_out_wait(5, r["ro"], r["rl"])
-    done = [local(r["rl"], res, r["osem"].at[0]), local(r["ll"], lgr, r["osem"].at[1])]
-    for c in done:
-        c.start()
+    done[0].start()
     job_second(4, False)
     job_second(5, False)
     both = jnp.concatenate([job_second_sum(4), job_second_sum(5)], axis=1)

time: 110 us -> 110 us (level)
  no operation moved by 1% of the time
where the time goes in v7:
time: 110 us
  Pallas kernels  109 us (99%)
    pallas_call x1, Pallas kernels, body(): pl.pallas_call(kernel, out_shape=shapes, in_specs=[anywhere] * 7, out_spe...  107 us

profile of v7, /device:TPU:0, one launch (start us, length us, event | category | flops | bytes accessed | tf_op | source)
XLA Modules:
  0.0 110.3 jit_solution(5375971230043959366)
XLA Ops:
  0.6 107.5 %block.1 = (bf16[2,8,8,1152]{3,2,1,0:T(8,128)(2,1)}, bf16[2,8,8,1152]{3,2,1,0:T(8,128)(2,1)}, bf16[36,1152]{1,0:T(8,128)(2,1)}, bf16[36,1152]{1,0:T(8,128)(2,1)}...) custom-call(bf16[2,8,8,1152]{3,2,1,0:T(8,128)(2,1)} %bitcast.12, bf16[2,8,8,1152]{3,2,1,0:T(8,128)(2,1)} %bitcast.13, ...), custom_call_target="tpu_custom_call" | custom-call | tf_op jit(solution)/shard_map/block/pallas_call | solution.py:738
  108.1 2.0 %hand_over.1 = (bf16[2,8,8,1152]{3,2,1,0:T(8,128)(2,1)}, bf16[2,8,8,1152]{3,2,1,0:T(8,128)(2,1)}, bf16[36,1152]{1,0:T(8,128)(2,1)}, bf16[36,1152]{1,0:T(8,128)(2...) custom-call(bf16[2,8,8,1152]{3,2,1,0:T(8,128)(2,1)} %get-tuple-element.18.refs_0_, ...), custom_call_target="tpu_custom_call" | custom-call | tf_op jit(solution)/shard_map/hand_over/pallas_call | solution.py:755

commit v8 on v6

--- a/solution.py
+++ b/solution.py
@@ -144,6 +144,13 @@
     peers += [z_peer(1), z_peer(3)]
     for where in peers:
         pl.semaphore_signal(barrier, inc=1, device_id=where, device_id_type=MESH)
+    for c in weights:
+        c.start()
+    for j in range(3):
+        r["win"][j, W:] = jnp.zeros((WP - W, D), BF16)
+    for k in range(4):
+        r["wo"][k, 36:] = jnp.zeros((12, 8, D), BF16)
+    r["dqc"][:, :, 768:] = jnp.zeros((4, 128, 128), BF16)
     pl.semaphore_wait(barrier, len(peers))
 
     def hop(ph, buf, parts, n, src=None):
@@ -299,13 +306,6 @@
     exchange_in(0, lat, r["xs"])
     share_start()
     gather_start(1, r["cy"], PARTS_C, cot, (0, 2))
-    for c in weights[:4]:
-        c.start()
-    for j in range(3):
-        r["win"][j, W:] = jnp.zeros((WP - W, D), BF16)
-    for k in range(4):
-        r["wo"][k, 36:] = jnp.zeros((12, 8, D), BF16)
-    r["dqc"][:, :, 768:] = jnp.zeros((4, 128, 128), BF16)
 
     mod_copy.wait()
     exchange_in_wait(0, lat, r["xs"])
@@ -313,8 +313,6 @@
         normed, _ = norm(halves(r["xs"], h))
         r["f"][0, 64 * h : 64 * h + 64, :] = (normed * (1.0 + row(1)) + row(0)).astype(BF16)
     gather_start(0, r["f"], PARTS_T)
-    for c in weights[4:]:
-        c.start()
     share_second()
     exchange_in(3, cot, r["cg"].at[0])
     for c in weights[:4]:

time: 110 us -> 110 us (level)
  no operation moved by 1% of the time
where the time goes in v8:
time: 110 us
  Pallas kernels  109 us (99%)
    pallas_call x1, Pallas kernels, body(): pl.pallas_call(kernel, out_shape=shapes, in_specs=[anywhere] * 7, out_spe...  107 us

profile of v8, /device:TPU:0, one launch (start us, length us, event | category | flops | bytes accessed | tf_op | source)
XLA Modules:
  0.0 110.2 jit_solution(18039606405321586324)
XLA Ops:
  0.6 107.4 %block.1 = (bf16[2,8,8,1152]{3,2,1,0:T(8,128)(2,1)}, bf16[2,8,8,1152]{3,2,1,0:T(8,128)(2,1)}, bf16[36,1152]{1,0:T(8,128)(2,1)}, bf16[36,1152]{1,0:T(8,128)(2,1)}...) custom-call(bf16[2,8,8,1152]{3,2,1,0:T(8,128)(2,1)} %bitcast.12, bf16[2,8,8,1152]{3,2,1,0:T(8,128)(2,1)} %bitcast.13, ...), custom_call_target="tpu_custom_call" | custom-call | tf_op jit(solution)/shard_map/block/pallas_call | solution.py:736
  108.1 2.0 %hand_over.1 = (bf16[2,8,8,1152]{3,2,1,0:T(8,128)(2,1)}, bf16[2,8,8,1152]{3,2,1,0:T(8,128)(2,1)}, bf16[36,1152]{1,0:T(8,128)(2,1)}, bf16[36,1152]{1,0:T(8,128)(2...) custom-call(bf16[2,8,8,1152]{3,2,1,0:T(8,128)(2,1)} %get-tuple-element.18.refs_0_, ...), custom_call_target="tpu_custom_call" | custom-call | tf_op jit(solution)/shard_map/hand_over/pallas_call | solution.py:753
